TPU v7x, 32 devices: a whole 2x2x4 slice. The times are simulated.
32 devices in a mesh: row: 4 (over x, core), seq: 8 (over z, y).
Axes of the slice: x: 2, y: 2, z: 4, core: 2. Of those that a mesh axis runs over, the one named last changes fastest.
Arguments:
- tokens_in: bfloat16 [4, 2048, 1024], P('row', 'seq'), may hold values from -6 to 6
- segment_ids: int32 [4, 2048], P('row'), may hold values from 0 to 15, never falling along the last dimension, each value on 1 to 1024 neighbouring positions
- norm_in_gain: float32 [1024], replicated, may hold values from 0.5 to 1.5
- query_weight: bfloat16 [1024, 1024], replicated, may hold values from -0.1875 to 0.1875
- key_weight: bfloat16 [1024, 1024], replicated, may hold values from -0.1875 to 0.1875
- value_weight: bfloat16 [1024, 1024], replicated, may hold values from -0.1875 to 0.1875
- rate_weight: bfloat16 [1024, 16], replicated, may hold values from -0.1875 to 0.1875
- gate_weight: bfloat16 [1024, 1024], replicated, may hold values from -0.1875 to 0.1875
- out_weight: bfloat16 [1024, 1024], replicated, may hold values from -0.1875 to 0.1875
- state_init: float32 [16, 64, 64], P('seq'), may hold values from -0.75 to 0.75
- offset_init: float32 [16, 64], P('seq'), may hold values from -3 to 3
- inner_gain: float32 [16, 64], P('seq'), may hold values from 0.5 to 1.5
- inner_shift: float32 [16, 64], P('seq'), may hold values from -3 to 3
- rate_bias: float32 [16], P('seq'), may hold values from -2 to 2
- norm_post_gain: float32 [1024], replicated, may hold values from 0.5 to 1.5
- norm_mlp_gain: float32 [1024], replicated, may hold values from 0.5 to 1.5
- ffn_gate: bfloat16 [1024, 2736], replicated, may hold values from -0.1875 to 0.1875
- ffn_up: bfloat16 [1024, 2736], replicated, may hold values from -0.1875 to 0.1875
- ffn_down: bfloat16 [2736, 1024], replicated, may hold values from -0.109375 to 0.109375
- cotangent: bfloat16 [4, 2048, 1024], P('row', 'seq'), may hold values from -6 to 6
Outputs:
- block_out: bfloat16 [4, 2048, 1024], P('row', 'seq')
- grad_tokens: float32 [4, 2048, 1024], P('row', 'seq')
- grad_norm_in: float32 [1024], P(('row', 'seq'))
- grad_query: float32 [1024, 1024], P(('row', 'seq'))
- grad_key: float32 [1024, 1024], P(('row', 'seq'))
- grad_value: float32 [1024, 1024], P(('row', 'seq'))
- grad_rate: float32 [1024, 16], P(('row', 'seq'))
- grad_gate: float32 [1024, 1024], P(('row', 'seq'))
- grad_out_proj: float32 [1024, 1024], P(('row', 'seq'))
- grad_state_init: float32 [16, 64, 64], P('seq')
- grad_offset_init: float32 [16, 64], P('seq')
- grad_inner_gain: float32 [16, 64], P('seq')
- grad_inner_shift: float32 [16, 64], P('seq')
- grad_rate_bias: float32 [16], P('seq')
- grad_norm_post: float32 [1024], P(('row', 'seq'))
- grad_norm_mlp: float32 [1024], P(('row', 'seq'))
- grad_ffn_gate: float32 [1024, 2736], P(('row', 'seq'))
- grad_ffn_up: float32 [1024, 2736], P(('row', 'seq'))
- grad_ffn_down: float32 [2736, 1024], P(None, ('row', 'seq'))
Inputs may be any that keep to these rules, and one draw needn't show every extreme that they name: Along a row segment_ids never fall; a document is a run of equal ids of at most 1024 tokens.
All inputs are finite; a program needn't handle non-finite values.
Results may differ from a plain program's by a relative error of at most 0.018.
Values may be sent and summed in bfloat16 or wider, within the bound.
A program may use at most 256 MiB of HBM per device.

v0:
```python
import jax
import jax.numpy as jnp
from jax import lax
from jax.sharding import PartitionSpec as P

MB = 16
MB_BLOCK = 8


EPS = 1e-06
BASE_LR = 1.0
HIGHEST = lax.Precision.HIGHEST


def layer_norm(values):
    center = values - jnp.mean(values, axis=-1, keepdims=True)
    inverse = lax.rsqrt(jnp.mean(center * center, axis=-1, keepdims=True) + EPS)
    return (center * inverse, inverse)


def mini_batch(
    carried,
    queries,
    keys_in,
    values_in,
    step_rate,
    segment,
    state_zero,
    offset_zero,
    norm_gain,
    norm_shift,
):
    weight, offset, last_seg = carried
    length = queries.shape[1]
    continues = (segment == last_seg[:, None]).astype(jnp.float32)[:, :, None]

    def starting(inputs):
        from_state = (
            jnp.einsum("bih,bhe->bie", inputs, weight, precision=HIGHEST) + offset[:, None, :]
        )
        from_zero = (
            jnp.einsum("bih,bhe->bie", inputs, state_zero, precision=HIGHEST)
            + offset_zero[:, None, :]
        )
        return continues * from_state + (1.0 - continues) * from_zero

    gain_row = norm_gain[:, None, :]
    shift_row = norm_shift[:, None, :]
    normed, inverse = layer_norm(starting(keys_in))
    residue = gain_row * normed + shift_row - (values_in - keys_in)
    scaled = residue * gain_row
    grad_inner = inverse * (
        scaled
        - jnp.mean(scaled, axis=-1, keepdims=True)
        - normed * jnp.mean(scaled * normed, axis=-1, keepdims=True)
    )
    positions = jnp.arange(length)
    causal = positions[None, :] <= positions[:, None]
    same_doc = (segment[:, :, None] == segment[:, None, :]) & causal[None, :, :]
    divisor = jnp.arange(1, length + 1).astype(jnp.float32)
    step_sizes = step_rate[:, None, :] / divisor[None, :, None] * same_doc.astype(jnp.float32)
    scores = jnp.einsum("bih,bjh->bij", queries, keys_in, precision=HIGHEST) + 1.0
    inner_out = starting(queries) - jnp.einsum(
        "bij,bjh->bih", step_sizes * scores, grad_inner, precision=HIGHEST
    )
    final_norm, unused = layer_norm(inner_out)
    results = queries + gain_row * final_norm + shift_row
    last_cont = continues[:, -1, :]
    last_steps = step_sizes[:, -1, :]
    base_weight = last_cont[:, :, None] * weight + (1.0 - last_cont[:, :, None]) * state_zero
    base_offset = last_cont * offset + (1.0 - last_cont) * offset_zero
    new_weight = base_weight - jnp.einsum(
        "bj,bjh,bje->bhe", last_steps, keys_in, grad_inner, precision=HIGHEST
    )
    new_offset = base_offset - jnp.einsum("bj,bje->be", last_steps, grad_inner, precision=HIGHEST)
    return ((new_weight, new_offset, segment[:, -1]), results)


def inner_loop(
    queries,
    keys_in,
    values_in,
    logits,
    segments,
    state_zero,
    offset_zero,
    norm_gain,
    norm_shift,
    rate_bias,
):
    batches, length, features = queries.shape
    block_len = MB * MB_BLOCK
    num_blocks = length // block_len
    step_rate = BASE_LR * jax.nn.sigmoid(logits + rate_bias[:, None]) / features

    def blocked(values):
        shaped = values.reshape((batches, num_blocks, block_len) + values.shape[2:])
        return jnp.swapaxes(shaped, 0, 1)

    def block_step(carried, inputs):
        query_blk, key_blk, value_blk, rate_blk, segment_blk = inputs
        pieces = []
        for number in range(MB_BLOCK):
            first_pos = number * MB
            last_pos = first_pos + MB
            carried, result = mini_batch(
                carried,
                query_blk[:, first_pos:last_pos],
                key_blk[:, first_pos:last_pos],
                value_blk[:, first_pos:last_pos],
                rate_blk[:, first_pos:last_pos],
                segment_blk[:, first_pos:last_pos],
                state_zero,
                offset_zero,
                norm_gain,
                norm_shift,
            )
            pieces.append(result)
        return (carried, jnp.concatenate(pieces, axis=1))

    stepper = jax.checkpoint(block_step)
    initial = (state_zero, offset_zero, jnp.full((batches,), -1, jnp.int32))
    unused, results = lax.scan(
        stepper,
        initial,
        (
            blocked(queries),
            blocked(keys_in),
            blocked(values_in),
            blocked(step_rate),
            blocked(segments),
        ),
    )
    return jnp.swapaxes(results, 0, 1).reshape(batches, length, features)


def rms_piece(values, gain):
    return values * lax.rsqrt(jnp.mean(values * values, axis=-1, keepdims=True) + EPS) * gain


def gelu_piece(values):
    return jax.nn.gelu(values, approximate=True)


def product(left, right):
    return jnp.dot(left, right, preferred_element_type=jnp.float32)


def outer_sum(left, right):
    return lax.dot_general(
        left, right, (((0,), (0,)), ((), ())), preferred_element_type=jnp.float32
    )


def back_product(left, right):
    return lax.dot_general(
        left, right, (((1,), (1,)), ((), ())), preferred_element_type=jnp.float32
    )


def shards(
    tokens_in,
    segment_ids,
    norm_in_gain,
    query_weight,
    key_weight,
    value_weight,
    rate_weight,
    gate_weight,
    out_weight,
    state_init,
    offset_init,
    inner_gain,
    inner_shift,
    rate_bias,
    norm_post_gain,
    norm_mlp_gain,
    ffn_gate,
    ffn_up,
    ffn_down,
    cotangent,
):
    row_count, token_count, features = tokens_in.shape
    groups = lax.axis_size("seq")
    heads_here = state_init.shape[0]
    head_size = state_init.shape[1]
    length = token_count * groups
    batches = row_count * heads_here
    flat_count = row_count * token_count
    flat_in = tokens_in.astype(jnp.float32).reshape(flat_count, features)
    normed_f, norm_in_pull = jax.vjp(rms_piece, flat_in, norm_in_gain)
    normed_in = normed_f.astype(jnp.bfloat16)

    def to_rows(values):
        return values.astype(jnp.bfloat16).reshape(row_count, token_count, values.shape[-1])

    q_heads, k_heads, v_heads, r_heads = (
        lax.all_to_all(
            to_rows(product(normed_in, query_weight)),
            "seq",
            split_axis=2,
            concat_axis=1,
            tiled=True,
        ),
        lax.all_to_all(
            to_rows(product(normed_in, key_weight)), "seq", split_axis=2, concat_axis=1, tiled=True
        ),
        lax.all_to_all(
            to_rows(product(normed_in, value_weight)),
            "seq",
            split_axis=2,
            concat_axis=1,
            tiled=True,
        ),
        lax.all_to_all(
            to_rows(product(normed_in, rate_weight)), "seq", split_axis=2, concat_axis=1, tiled=True
        ),
    )

    def by_head(values):
        shaped = values.astype(jnp.float32).reshape(row_count, length, heads_here, head_size)
        return jnp.transpose(shaped, (0, 2, 1, 3)).reshape(batches, length, head_size)

    def to_tokens(values):
        shaped = values.reshape(row_count, heads_here, length, head_size)
        return (
            jnp.transpose(shaped, (0, 2, 1, 3))
            .reshape(row_count, length, heads_here * head_size)
            .astype(jnp.bfloat16)
        )

    rate_in = jnp.transpose(r_heads.astype(jnp.float32), (0, 2, 1)).reshape(batches, length)
    seg_heads = jnp.broadcast_to(segment_ids[:, None, :], (row_count, heads_here, length)).reshape(
        batches, length
    )

    def per_batch(values):
        spread = values[None]
        return spread.reshape((batches,) + values.shape[1:])

    def mixer_fn(
        queries,
        keys_in,
        values_in,
        logits,
        state_zero,
        offset_zero,
        norm_gain,
        norm_shift,
        bias_rate,
    ):
        return inner_loop(
            queries,
            keys_in,
            values_in,
            logits,
            seg_heads,
            per_batch(state_zero),
            per_batch(offset_zero),
            per_batch(norm_gain),
            per_batch(norm_shift),
            per_batch(bias_rate),
        )

    mixed_heads, mixer_pull = jax.vjp(
        mixer_fn,
        by_head(q_heads),
        by_head(k_heads),
        by_head(v_heads),
        rate_in,
        state_init,
        offset_init,
        inner_gain,
        inner_shift,
        rate_bias,
    )
    mixed_tok = lax.all_to_all(
        to_tokens(mixed_heads), "seq", split_axis=1, concat_axis=2, tiled=True
    )
    mixed_f = mixed_tok.astype(jnp.float32).reshape(flat_count, features)
    post_norm, post_pull = jax.vjp(rms_piece, mixed_f, norm_post_gain)
    gate_pre = product(normed_in, gate_weight)
    gelu_out, gelu_pull = jax.vjp(gelu_piece, gate_pre)
    branch = (post_norm * gelu_out).astype(jnp.bfloat16)
    middle = flat_in + product(branch, out_weight)
    normed_mid_f, mid_pull = jax.vjp(rms_piece, middle, norm_mlp_gain)
    normed_mid = normed_mid_f.astype(jnp.bfloat16)
    gate_proj = product(normed_mid, ffn_gate)
    up_proj = product(normed_mid, ffn_up)
    silu_out, silu_pull = jax.vjp(jax.nn.silu, gate_proj)
    hidden = (silu_out * up_proj).astype(jnp.bfloat16)
    block_out = (middle + product(hidden, ffn_down)).astype(jnp.bfloat16)
    grad_out = cotangent.astype(jnp.float32).reshape(flat_count, features)
    grad_ffn = grad_out.astype(jnp.bfloat16)
    grad_down = outer_sum(hidden, grad_ffn)
    grad_hidden = back_product(grad_ffn, ffn_down)
    grad_gate_proj = silu_pull(grad_hidden * up_proj)[0].astype(jnp.bfloat16)
    grad_up_proj = (grad_hidden * silu_out).astype(jnp.bfloat16)
    grad_ffn_gate = outer_sum(normed_mid, grad_gate_proj)
    grad_ffn_up = outer_sum(normed_mid, grad_up_proj)
    grad_normed_mid = back_product(grad_gate_proj, ffn_gate) + back_product(grad_up_proj, ffn_up)
    grad_mid_part, grad_norm_mlp = mid_pull(grad_normed_mid)
    grad_middle = grad_out + grad_mid_part
    grad_branch_out = grad_middle.astype(jnp.bfloat16)
    grad_out_proj = outer_sum(branch, grad_branch_out)
    grad_branch = back_product(grad_branch_out, out_weight)
    grad_gate_pre = gelu_pull(grad_branch * post_norm)[0].astype(jnp.bfloat16)
    grad_gate = outer_sum(normed_in, grad_gate_pre)
    grad_mixed_part, grad_norm_post = post_pull(grad_branch * gelu_out)
    grad_mixed = grad_mixed_part.astype(jnp.bfloat16).reshape(row_count, token_count, features)
    grad_heads = lax.all_to_all(grad_mixed, "seq", split_axis=2, concat_axis=1, tiled=True)
    grad_q, grad_k, grad_v, grad_r, grad_state, grad_offset, grad_igain, grad_ishift, grad_rbias = (
        mixer_pull(by_head(grad_heads))
    )
    grad_rate_rows = jnp.transpose(grad_r.reshape(row_count, heads_here, length), (0, 2, 1)).astype(
        jnp.bfloat16
    )
    grad_q_tok, grad_k_tok, grad_v_tok, grad_r_tok = (
        lax.all_to_all(to_tokens(grad_q), "seq", split_axis=1, concat_axis=2, tiled=True),
        lax.all_to_all(to_tokens(grad_k), "seq", split_axis=1, concat_axis=2, tiled=True),
        lax.all_to_all(to_tokens(grad_v), "seq", split_axis=1, concat_axis=2, tiled=True),
        lax.all_to_all(grad_rate_rows, "seq", split_axis=1, concat_axis=2, tiled=True),
    )
    head_summed = lax.psum((grad_state, grad_offset, grad_igain, grad_ishift, grad_rbias), "row")
    grad_q_flat = grad_q_tok.reshape(flat_count, features)
    grad_k_flat = grad_k_tok.reshape(flat_count, features)
    grad_v_flat = grad_v_tok.reshape(flat_count, features)
    grad_r_flat = grad_r_tok.reshape(flat_count, grad_r_tok.shape[-1])
    grad_query = outer_sum(normed_in, grad_q_flat)
    grad_key = outer_sum(normed_in, grad_k_flat)
    grad_value = outer_sum(normed_in, grad_v_flat)
    grad_rate = outer_sum(normed_in, grad_r_flat)
    grad_normed_in = (
        back_product(grad_q_flat, query_weight)
        + back_product(grad_k_flat, key_weight)
        + back_product(grad_v_flat, value_weight)
        + back_product(grad_r_flat, rate_weight)
        + back_product(grad_gate_pre, gate_weight)
    )
    grad_in_part, grad_norm_in = norm_in_pull(grad_normed_in)
    grad_tokens = (grad_middle + grad_in_part).reshape(row_count, token_count, features)
    summed = (
        lax.psum_scatter(grad_norm_in, ("row", "seq"), scatter_dimension=0, tiled=True),
        lax.psum_scatter(grad_query, ("row", "seq"), scatter_dimension=0, tiled=True),
        lax.psum_scatter(grad_key, ("row", "seq"), scatter_dimension=0, tiled=True),
        lax.psum_scatter(grad_value, ("row", "seq"), scatter_dimension=0, tiled=True),
        lax.psum_scatter(grad_rate, ("row", "seq"), scatter_dimension=0, tiled=True),
        lax.psum_scatter(grad_gate, ("row", "seq"), scatter_dimension=0, tiled=True),
        lax.psum_scatter(grad_out_proj, ("row", "seq"), scatter_dimension=0, tiled=True),
        lax.psum_scatter(grad_norm_post, ("row", "seq"), scatter_dimension=0, tiled=True),
        lax.psum_scatter(grad_norm_mlp, ("row", "seq"), scatter_dimension=0, tiled=True),
        lax.psum_scatter(grad_ffn_gate, ("row", "seq"), scatter_dimension=0, tiled=True),
        lax.psum_scatter(grad_ffn_up, ("row", "seq"), scatter_dimension=0, tiled=True),
        lax.psum_scatter(grad_down, ("row", "seq"), scatter_dimension=1, tiled=True),
    )
    return (
        block_out.reshape(row_count, token_count, features),
        grad_tokens,
        summed[0],
        summed[1],
        summed[2],
        summed[3],
        summed[4],
        summed[5],
        summed[6],
        head_summed[0],
        head_summed[1],
        head_summed[2],
        head_summed[3],
        head_summed[4],
        summed[7],
        summed[8],
        summed[9],
        summed[10],
        summed[11],
    )


def solution(mesh):
    placed = (
        P("row", "seq", None),
        P("row", None),
        P(),
        P(),
        P(),
        P(),
        P(),
        P(),
        P(),
        P("seq", None, None),
        P("seq", None),
        P("seq", None),
        P("seq", None),
        P("seq"),
        P(),
        P(),
        P(),
        P(),
        P(),
        P("row", "seq", None),
    )
    return jax.shard_map(
        shards,
        mesh=mesh,
        in_specs=placed,
        out_specs=(
            P("row", "seq", None),
            P("row", "seq", None),
            P(("row", "seq")),
            P(("row", "seq"), None),
            P(("row", "seq"), None),
            P(("row", "seq"), None),
            P(("row", "seq"), None),
            P(("row", "seq"), None),
            P(("row", "seq"), None),
            P("seq", None, None),
            P("seq", None),
            P("seq", None),
            P("seq", None),
            P("seq"),
            P(("row", "seq")),
            P(("row", "seq")),
            P(("row", "seq"), None),
            P(("row", "seq"), None),
            P(None, ("row", "seq")),
        ),
        check_vma=False,
    )
```

profile of v0, /device:TPU:0, one launch (start us, length us, event | category | flops | bytes accessed | tf_op | source)
XLA Modules:
  0.0 3546.4 jit_solution(11066524977128149193)
XLA Ops:
  12.4 7.3 all-to-all-start
  24.2 4.8 reduce.117
  30.6 6.0 all-to-all-start.1
  39.7 3.6 copy.581
  43.3 5.6 reduce.118
  50.8 6.3 all-to-all-start.2
  60.2 3.6 copy.583
  63.8 5.6 reduce.119
  71.4 6.0 all-to-all-start.3
  105.0 3.5 reshape.1969
  121.1 450.2 %while.58 = (s32[]{:T(128)}, f32[2,64,64]{2,1,0:T(8,128)S(1)}, f32[2,64]{1,0:T(2,128)S(1)}, s32[2]{0:T(128)S(1)}, bf16[16,2,128,64]{3,2,1,0:T(8,128)(2,1)}, /*in...) while((s32[]{:T(128)}, f32[2,64,64]{2,1,0:T(8,128)S(1)}, ...), condition=%wide.region_50.51_spmd.clone.clone, body=%wide.region_1.50_spmd.clone.clone.sunk | while | flops 70383152 | bytes 7373821 | solution.py:123
  575.8 3.6 copy.590
  579.4 13.4 reduce.120
  594.7 18.5 all_to_all.118
  613.2 3.5 reshape.1971
  630.5 4.2 multiply_convert_fusion
  645.3 3.6 copy.593
  648.9 5.6 reduce.121
  656.4 4.1 all-to-all-start.5
  660.6 12.8 all-to-all-done.5
  673.4 3.5 reshape.1973
  688.8 1201.8 %while.59 = (s32[]{:T(128)}, f32[2,64]{1,0:T(2,128)}, f32[2,64]{1,0:T(2,128)}, f32[2,64,64]{2,1,0:T(8,128)S(1)}, f32[2,64]{1,0:T(2,128)}, /*index=5*/f32[2,64,64...) while((s32[]{:T(128)}, f32[2,64]{1,0:T(2,128)}, ...), condition=%wide.region_241.242_spmd.clone, body=%wide.region_56.241_spmd.clone.sunk | while | flops 210075968 | bytes 18414552 | solution.py:123
  1894.3 13.4 reduce.125
  1909.4 10.0 all_to_all.114
  1929.4 4.0 fusion.932
  1936.1 3.7 copy.601
  1939.9 12.6 reduce.122
  1953.3 16.6 all_to_all.115
  1980.8 3.6 copy.604
  1984.3 12.6 reduce.123
  1997.8 17.4 all_to_all.116
  2026.0 3.6 copy.607
  2029.6 12.6 reduce.124
  2043.1 17.9 all_to_all.117
  2070.1 7.4 fusion.1048
  2077.6 7.3 fusion.1049
  2086.0 7.3 fusion.927
  2096.1 5.2 fusion.904
  2102.1 12.3 all-reduce.44
  2123.0 40.3 %all-reduce.43 = (f32[1024]{0:T(1024)S(1)}, f32[1024]{0:T(1024)S(1)}, f32[1024]{0:T(1024)S(1)}) all-reduce(f32[1024]{0:T(1024)S(1)} %get-tuple-element.1547, f32[1024]{0:T(1024)S(1)} %copy-done.62, f32[1024]{0:T(1024)S(1)} %copy-done.55), channel_id=2, replica_groups=mesh['row'=4,'seq'=8] {'row','seq'}, use_global_device_ids=true, to_apply=%region_244.245.clone | all-reduce | flops 3072 | bytes 24576
  2167.8 36.5 %reduce-scatter.18.cloned.1.call-done = f32[32,1024]{1,0:T(8,128)} async-done(((f32[1024,1024]{1,0:T(8,128)}), f32[32,1024]{1,0:T(8,128)}) %reduce-scatter.18.cloned.1.call-update) | async-done | bytes 131088 | tf_op jit(solution)/shard_map/reduce_scatter | solution.py:348
  2204.3 146.3 %reduce-scatter.20.cloned.1.call-done = f32[32,1024]{1,0:T(8,128)} async-done(((f32[1024,1024]{1,0:T(8,128)}), f32[32,1024]{1,0:T(8,128)}) %reduce-scatter.20.cloned.1.call-update) | async-done | bytes 131088 | tf_op jit(solution)/shard_map/reduce_scatter | solution.py:349
  2350.6 145.0 %reduce-scatter.12.cloned.1.call-done = f32[32,1024]{1,0:T(8,128)} async-done(((f32[1024,1024]{1,0:T(8,128)}), f32[32,1024]{1,0:T(8,128)}) %reduce-scatter.12.cloned.1.call-update) | async-done | bytes 131088 | tf_op jit(solution)/shard_map/reduce_scatter | solution.py:344
  2495.6 145.9 %reduce-scatter.14.cloned.1.call-done = f32[32,1024]{1,0:T(8,128)} async-done(((f32[1024,1024]{1,0:T(8,128)}), f32[32,1024]{1,0:T(8,128)}) %reduce-scatter.14.cloned.1.call-update) | async-done | bytes 131088 | tf_op jit(solution)/shard_map/reduce_scatter | solution.py:345
  2641.4 146.0 %reduce-scatter.16.cloned.1.call-done = f32[32,1024]{1,0:T(8,128)} async-done(((f32[1024,1024]{1,0:T(8,128)}), f32[32,1024]{1,0:T(8,128)}) %reduce-scatter.16.cloned.1.call-update) | async-done | bytes 131088 | tf_op jit(solution)/shard_map/reduce_scatter | solution.py:346
  2787.5 249.2 %reduce-scatter.22.cloned.1.call-done = f32[32,2736]{1,0:T(8,128)} async-done(((f32[1024,2736]{1,0:T(8,128)}), f32[32,2736]{1,0:T(8,128)}) %reduce-scatter.22.cloned.1.call-update) | async-done | bytes 350224 | tf_op jit(solution)/shard_map/reduce_scatter | solution.py:352
  3036.7 251.7 %reduce-scatter.24.cloned.1.call-done = f32[32,2736]{1,0:T(8,128)} async-done(((f32[1024,2736]{1,0:T(8,128)}), f32[32,2736]{1,0:T(8,128)}) %reduce-scatter.24.cloned.1.call-update) | async-done | bytes 350224 | tf_op jit(solution)/shard_map/reduce_scatter | solution.py:353
  3288.3 251.1 %reduce-scatter.26.cloned.1.call-done = f32[2736,32]{0,1:T(8,128)} async-done(((f32[2736,1024]{0,1:T(8,128)}), f32[2736,32]{0,1:T(8,128)}) %reduce-scatter.26.cloned.1.call-update) | async-done | bytes 350224 | tf_op jit(solution)/shard_map/reduce_scatter | solution.py:354
  (10292 shorter events, 1798.2 us)
Async XLA Ops:
  7.2 613.0 %copy-start = (bf16[1024,1024]{1,0:T(8,128)(2,1)S(1)}, bf16[1024,1024]{1,0:T(8,128)(2,1)}, u32[]{:S(2)}) copy-start(bf16[1024,1024]{1,0:T(8,128)(2,1)} %param.31) | copy-start | bytes 6291460
  9.2 47.9 %copy-start.39 = (f32[256]{0:T(256)}, f32[256]{0:T(256)S(1)}, u32[]{:S(2)}) copy-start(f32[256]{0:T(256)S(1)} %fusion.949) | copy-start | bytes 3076
  12.4 17.6 all-to-all-start
  24.2 12.3 copy-start.4
  24.2 12.3 copy-start.34
  30.6 20.2 all-to-all-start.1
  50.8 20.6 all-to-all-start.2
  63.8 13.6 copy-start.1
  63.8 13.6 copy-start.2
  63.8 13.7 copy-start.54
  63.8 13.7 copy-start.59
  71.4 33.6 all-to-all-start.3
  625.3 13.6 copy-start.5
  656.4 17.0 all-to-all-start.5
  660.5 1453.9 %reduce-scatter.28.cloned.1.call-start = ((), (), s32[]{:S(2)}) async-start(), calls=%async_computation.27 | async-start | bytes 540672
  734.4 8.1 copy-start.49
  740.2 9.4 copy-start.46
  815.3 9.4 copy-start.46
  884.6 8.1 copy-start.49
  890.4 9.4 copy-start.46
  959.8 8.1 copy-start.49
  965.6 9.4 copy-start.46
  1040.7 9.4 copy-start.46
  1115.8 9.4 copy-start.46
  1190.9 9.4 copy-start.46
  1266.0 9.4 copy-start.46
  1341.1 9.4 copy-start.46
  1410.4 8.1 copy-start.49
  1416.2 9.4 copy-start.46
  1491.4 9.4 copy-start.46
  1566.5 9.4 copy-start.46
  1641.6 9.4 copy-start.46
  1716.7 9.4 copy-start.46
  1791.9 9.4 copy-start.46
  1867.0 9.4 copy-start.46
  1894.3 29.8 copy-start.35
  1894.3 29.8 copy-start.41
  1907.7 17.7 copy-start.14
  1925.4 279.0 %reduce-scatter.18.cloned.1.call-start = ((), (), s32[]{:S(2)}) async-start(), calls=%async_computation.22 | async-start | bytes 4325376 | tf_op jit(solution)/shard_map/reduce_scatter | solution.py:348
  1928.3 422.2 %reduce-scatter.20.cloned.1.call-start = ((), (), s32[]{:S(2)}) async-start(), calls=%async_computation.23 | async-start | bytes 4325376 | tf_op jit(solution)/shard_map/reduce_scatter | solution.py:349
  1933.4 562.2 %reduce-scatter.12.cloned.1.call-start = ((), (), s32[]{:S(2)}) async-start(), calls=%async_computation.19 | async-start | bytes 4325376 | tf_op jit(solution)/shard_map/reduce_scatter | solution.py:344
  1978.0 663.5 %reduce-scatter.14.cloned.1.call-start = ((), (), s32[]{:S(2)}) async-start(), calls=%async_computation.20 | async-start | bytes 4325376 | tf_op jit(solution)/shard_map/reduce_scatter | solution.py:345
  2023.3 764.2 %reduce-scatter.16.cloned.1.call-start = ((), (), s32[]{:S(2)}) async-start(), calls=%async_computation.21 | async-start | bytes 4325376 | tf_op jit(solution)/shard_map/reduce_scatter | solution.py:346
  2069.1 967.5 %reduce-scatter.22.cloned.1.call-start = ((), (), s32[]{:S(2)}) async-start(), calls=%async_computation.24 | async-start | bytes 11894784 | tf_op jit(solution)/shard_map/reduce_scatter | solution.py:352
  2077.6 1210.7 %reduce-scatter.24.cloned.1.call-start = ((), (), s32[]{:S(2)}) async-start(), calls=%async_computation.25 | async-start | bytes 11894784 | tf_op jit(solution)/shard_map/reduce_scatter | solution.py:353
  2085.0 1454.4 %reduce-scatter.26.cloned.1.call-start = ((), (), s32[]{:S(2)}) async-start(), calls=%async_computation.26 | async-start | bytes 11894784 | tf_op jit(solution)/shard_map/reduce_scatter | solution.py:354
  2096.1 19.8 copy-start.17
  2121.4 43.6 %copy-start.57 = (f32[256]{0:T(256)S(1)}, f32[256]{0:T(256)}, u32[]{:S(2)}) copy-start(f32[256]{0:T(256)} %copy-done.56) | copy-start | bytes 3076
  (125 other events, 730.4 us)
Sparse Core Ops, SparseCore 0:
  1925.5 133.5 reduce-scatter.27
  2061.9 142.3 reduce-scatter.17
  2207.2 143.3 reduce-scatter.19
  2353.3 142.2 reduce-scatter.11
  2498.3 143.1 reduce-scatter.13
  2644.2 143.2 reduce-scatter.15
  2790.3 246.2 reduce-scatter.21
  3039.5 248.7 reduce-scatter.23
  3291.2 248.1 reduce-scatter.25
where the time goes:
time: 3560 us; the launch traced here: 3550 us
  waiting for transfers between devices  1380 us (39%)
  matrix products  1060 us (30%)
  other arithmetic  477 us (13%)
  local copies, waits for them, and re-layouts  414 us (12%)
  blocking collectives  133 us (4%)
    dot_general x1024, matrix products, starting(): jnp.einsum('bih,bhe->bie', inputs, state_zero, precision=HIGHEST)  269 us
    reduce_scatter x1, waiting for transfers between devices, shards(): lax.psum_scatter(grad_ffn_up, ('row', 'seq'), scatter_dimension=0, tiled=...  252 us
    reduce_scatter x1, waiting for transfers between devices, shards(): lax.psum_scatter(grad_down, ('row', 'seq'), scatter_dimension=1, tiled=True)  251 us
    reduce_scatter x1, waiting for transfers between devices, shards(): lax.psum_scatter(grad_ffn_gate, ('row', 'seq'), scatter_dimension=0, tile...  249 us
    dot_general x1024, matrix products, starting(): jnp.einsum('bih,bhe->bie', inputs, weight, precision=HIGHEST)  240 us
    dot_general x496, matrix products, mini_batch(): jnp.einsum('bj,bjh,bje->bhe', last_steps, keys_in, grad_inner, precision=...  154 us
    squeeze x192, local copies, waits for them, and re-layouts, inner_loop(): lax.scan(stepper, initial, (blocked(queries), blocked(keys_in), blocked(v...  154 us
    dot_general x512, matrix products, mini_batch(): jnp.einsum('bij,bjh->bih', step_sizes * scores, grad_inner, precision=HIG...  149 us

commit v1 on v0

v1 whole, which is shorter than its diff:
```python
import functools
import jax
import jax.numpy as jnp
import numpy as np
from jax import lax
from jax.experimental import pallas as pl
from jax.experimental.pallas import tpu as pltpu
from jax.sharding import PartitionSpec as P

MB = 16
BLK = 128
EPS = 1e-06
F32 = jnp.float32
BF = jnp.bfloat16


def dot(a, b):
    return lax.dot_general(a, b, (((1,), (0,)), ((), ())), preferred_element_type=F32)


def dot_nt(a, b):
    return lax.dot_general(a, b, (((1,), (1,)), ((), ())), preferred_element_type=F32)


def dot_tn(a, b):
    return lax.dot_general(a, b, (((0,), (0,)), ((), ())), preferred_element_type=F32)


def split(x):
    hi = x.astype(BF)
    return hi, (x - hi.astype(F32)).astype(BF)


def head_blocks(lanes, size):
    shape = (lanes, lanes)
    return lax.broadcasted_iota(jnp.int32, shape, 0) // size == lax.broadcasted_iota(jnp.int32, shape, 1) // size


def mean_matrix(lanes, size):
    return jnp.where(head_blocks(lanes, size), 1.0 / size, 0.0).astype(BF)


def head_mean(x, means):
    hi, lo = split(x)
    return dot(hi, means) + dot(lo, means)


def lane_mean(x, size):
    lanes = x.shape[-1]
    if lanes == size:
        return jnp.sum(x, axis=-1, keepdims=True) * (1.0 / size)
    at = lax.broadcasted_iota(jnp.int32, x.shape, 1) // size
    out = None
    for h in range(lanes // size):
        part = jnp.sum(jnp.where(at == h, x, 0.0), axis=-1, keepdims=True) * (1.0 / size)
        out = part if out is None else jnp.where(at == h, part, out)
    return out


def lane_schedule(segments):
    count = segments.shape[0] // MB
    last = segments[MB - 1::MB]
    before = jnp.concatenate([jnp.full((1,), -1, jnp.int32), last[:-1]])
    fresh = last != before
    at = jnp.arange(count, dtype=jnp.int32)
    first, stop = at[:, None], at[None, :] + 1
    stop_ok = jnp.concatenate([fresh[1:], jnp.ones((1,), bool)])
    steps0 = first + 1 + count - stop
    steps1 = jnp.where(stop < count, stop - first + 1, count - first)
    cost = jnp.where(fresh[:, None] & stop_ok[None, :] & (stop > first), jnp.maximum(steps0, steps1), 4 * count)
    best = jnp.argmin(cost.reshape(-1)).astype(jnp.int32)
    a, b = best // count, best % count + 1
    end = jnp.minimum(b, count - 1)
    steps = jnp.maximum(a + 1 + count - b, end - a + 1)
    t = jnp.arange(count + 2, dtype=jnp.int32)
    per = BLK // MB

    def table(where, valid, owned, edge):
        where_ok = jnp.where(valid, where, count - 1)
        write = jnp.where(valid & owned, where, count)
        slot = jnp.where(valid & owned & (where % per == edge), where // per, count // per)
        return jnp.stack([where_ok, write, slot])

    f0 = jnp.where(t <= a, t, t - a - 1 + b)
    f1 = a + t
    fwd = jnp.stack([table(f0, f0 < count, (t <= a) | (f0 > b), 0), table(f1, f1 <= end, f1 > a, 0)])
    r0 = jnp.where(t < count - b, count - 1 - t, a - (t - (count - b)))
    r1 = end - t
    bwd = jnp.stack([table(r0, r0 >= 0, (r0 >= b) | (r0 < a), per - 1), table(r1, r1 >= a, r1 < b, per - 1)])
    return steps.reshape(1), fwd, bwd, jnp.concatenate([jnp.full((1,), -1, jnp.int32), last])


def scan_fwd_kernel(size, mean_of, steps_ref, table_ref, last_ref, k_ref, v_ref, seg_ref, rate_ref, wz_ref, bz_ref, gain_ref, shift_ref,
                    z_ref, g_ref, s_ref, b_ref, z0_ref, pd_ref, m5_ref, zb_ref, gb_ref, sw_ref, s2_ref, bw_ref):
    tokens, lanes = k_ref.shape
    count = tokens // MB
    mask = head_blocks(lanes, size)
    means = mean_matrix(lanes, size)
    gain, shift = gain_ref[...], shift_ref[...]
    gain2 = gain * gain
    wz_hi, wz_lo = split(wz_ref[...])
    bz = bz_ref[...]

    @pl.loop(0, tokens // 256)
    def _(n):
        rows = pl.ds(pl.multiple_of(n * 256, 256), 256)
        k = k_ref[rows, :]
        z0_ref[rows, :] = dot(k, wz_hi) + dot(k, wz_lo) + bz
        pd = gain * (shift - (v_ref[rows, :].astype(F32) - k.astype(F32)))
        pd_ref[rows, :] = pd
        m5_ref[rows, :] = head_mean(pd, means)

    sw_ref[...] = jnp.zeros_like(sw_ref)
    s2_ref[...] = jnp.zeros_like(s2_ref)
    bw_ref[...] = jnp.zeros_like(bw_ref)

    def step(t, carry):
        for lane in range(2):
            m, write, slot = table_ref[lane, 0, t], table_ref[lane, 1, t], table_ref[lane, 2, t]
            rows = pl.ds(pl.multiple_of(m * MB, MB), MB)
            to = pl.ds(pl.multiple_of(write * MB, MB), MB)
            last_before, last_here = last_ref[m], last_ref[m + 1]
            k = k_ref[rows, :]
            seg = seg_ref[rows, :]
            bias = bw_ref[lane, 0:1, :]
            state = sw_ref[lane]
            s_ref[slot] = state
            b_ref[slot] = bw_ref[lane]
            zc = dot(jnp.concatenate([k, k], axis=1), s2_ref[lane]) + bias
            z = z0_ref[rows, :] + jnp.where(seg == last_before, zc, 0.0)
            pd = pd_ref[rows, :]
            gz = gain2 * z
            q1, q2, q3, q4 = mean_of(z * z), mean_of(gz), mean_of(gz * z), mean_of(pd * z)
            s = lax.rsqrt(q1 + EPS)
            m1 = s * q2 + m5_ref[rows, :]
            m2 = s * (s * q3 + q4)
            g = s * ((gain2 - m2) * (s * z) + (pd - m1))
            rho = jnp.where(seg == last_here, rate_ref[rows, :], 0.0) * (1.0 / MB)
            step_g = rho * g
            zb_ref[to, :] = z
            gb_ref[to, :] = g
            hi, lo = split(step_g)
            delta = dot_tn(jnp.concatenate([k, k], axis=0), jnp.concatenate([hi, lo], axis=0))
            keep = jnp.where(last_before == last_here, 1.0, 0.0)
            state = keep * state - jnp.where(mask, delta, 0.0)
            sw_ref[lane] = state
            s_hi, s_lo = split(state)
            s2_ref[lane] = jnp.concatenate([s_hi, s_lo], axis=0)
            bw_ref[lane] = keep * bw_ref[lane] - jnp.sum(step_g, axis=0, keepdims=True)
        return carry

    lax.fori_loop(0, steps_ref[0], step, 0)
    z_ref[...] = zb_ref[0:tokens, :]
    g_ref[...] = gb_ref[0:tokens, :]


def smem():
    return pl.BlockSpec(memory_space=pltpu.SMEM)


def vmem():
    return pl.BlockSpec(memory_space=pltpu.VMEM)


def scan_fwd(schedule, k, v, seg, rate, wz, bz, gain, shift, size, mean_of):
    steps, table, _, last = schedule
    tokens, lanes = k.shape
    blocks = tokens // BLK
    return pl.pallas_call(
        functools.partial(scan_fwd_kernel, size, mean_of),
        out_shape=(
            jax.ShapeDtypeStruct((tokens, lanes), F32),
            jax.ShapeDtypeStruct((tokens, lanes), F32),
            jax.ShapeDtypeStruct((blocks + 1, lanes, lanes), F32),
            jax.ShapeDtypeStruct((blocks + 1, 8, lanes), F32),
        ),
        in_specs=[smem()] * 3 + [vmem()] * 8,
        out_specs=(vmem(),) * 4,
        scratch_shapes=[
            pltpu.VMEM((tokens, lanes), F32),
            pltpu.VMEM((tokens, lanes), F32),
            pltpu.VMEM((tokens, lanes), F32),
            pltpu.VMEM((tokens + MB, lanes), F32),
            pltpu.VMEM((tokens + MB, lanes), F32),
            pltpu.VMEM((2, lanes, lanes), F32),
            pltpu.VMEM((2, 2 * lanes, lanes), BF),
            pltpu.VMEM((2, 8, lanes), F32),
        ],
        compiler_params=pltpu.CompilerParams(vmem_limit_bytes=60 * 1024 * 1024),
        name="scan_fwd",
    )(steps, table, last, k, v, seg, rate, wz, bz, gain, shift)


def weights_of(segments):
    blocks = segments.shape[0] // BLK
    seg = segments.reshape(blocks, BLK)
    same = seg[:, :, None] == seg[:, None, :]
    at = jnp.arange(BLK)
    mb = at // MB
    inside = (mb[:, None] == mb[None, :]) & (at[None, :] <= at[:, None])
    part = inside / (at % MB + 1).astype(F32)[:, None] + (mb[None, :] < mb[:, None]) * (1.0 / MB)
    return (same * part[None]).astype(F32).reshape(blocks * BLK, BLK)


def head_masks(shape, size):
    at = lax.broadcasted_iota(jnp.int32, shape, 1) // size
    return [at == h for h in range(shape[1] // size)]


def only(mask, x):
    return jnp.where(mask, x, jnp.zeros_like(x))


def layer_norm_parts(o, means):
    center = o - head_mean(o, means)
    inverse = lax.rsqrt(head_mean(center * center, means) + EPS)
    return center * inverse, inverse


def out_fwd_kernel(size, seg_before_ref, q_ref, k_ref, g_ref, rate_ref, seg_ref, w_ref, s_ref, b_ref, wz_ref, bz_ref, gain_ref, shift_ref,
                   mixed_ref, fin_ref, inv_ref):
    n = pl.program_id(0)
    lanes = q_ref.shape[1]
    means = mean_matrix(lanes, size)
    q, k = q_ref[...], k_ref[...]
    gr = (rate_ref[...] * g_ref[...])
    w = w_ref[...]
    wz_hi, wz_lo = split(wz_ref[...])
    s_hi, s_lo = split(s_ref[0])
    o = dot(q, wz_hi) + dot(q, wz_lo) + bz_ref[...]
    o += jnp.where(seg_ref[...] == seg_before_ref[n], dot(q, s_hi) + dot(q, s_lo) + b_ref[0, 0:1, :], 0.0)
    g_hi, g_lo = split(gr)
    for mine in head_masks(q.shape, size):
        a = w * (dot_nt(only(mine, q), k) + 1.0)
        a_hi, a_lo = split(a)
        gh, gl = only(mine, g_hi), only(mine, g_lo)
        o -= dot(a_hi, gh) + dot(a_lo, gh) + dot(a_hi, gl)
    fin, inverse = layer_norm_parts(o, means)
    mixed_ref[...] = (q.astype(F32) + gain_ref[...] * fin + shift_ref[...]).astype(BF)
    fin_ref[...] = fin
    inv_ref[...] = inverse


def rows_spec(lanes):
    return pl.BlockSpec((BLK, lanes), lambda n: (n, 0))


def state_spec(*shape):
    return pl.BlockSpec((1,) + shape, lambda n: (n, 0, 0))


def whole(*shape):
    return pl.BlockSpec(shape, lambda n: (0,) * len(shape))


def out_fwd(seg_before, q, k, g, rate, seg, w, states, biases, wz, bz, gain, shift, size):
    tokens, lanes = q.shape
    rows = rows_spec(lanes)
    return pl.pallas_call(
        functools.partial(out_fwd_kernel, size),
        grid=(tokens // BLK,),
        out_shape=(
            jax.ShapeDtypeStruct((tokens, lanes), BF),
            jax.ShapeDtypeStruct((tokens, lanes), F32),
            jax.ShapeDtypeStruct((tokens, lanes), F32),
        ),
        in_specs=[smem(), rows, rows, rows, rows, rows, rows_spec(BLK), state_spec(lanes, lanes), state_spec(8, lanes),
                  whole(lanes, lanes), whole(1, lanes), whole(1, lanes), whole(1, lanes)],
        out_specs=(rows,) * 3,
        name="out_fwd",
    )(seg_before, q, k, g, rate, seg, w, states, biases, wz, bz, gain, shift)


def out_bwd_kernel(size, seg_before_ref, dmix_ref, q_ref, k_ref, v_ref, z_ref, g_ref, rate_ref, seg_ref, w_ref, s_ref, fin_ref, inv_ref, wz_ref, gain_ref, shift_ref,
                   dq_ref, do_ref, dgo_ref, alpha_ref, p_ref, p2_ref, n_ref, n2_ref, sn_ref, dgain_ref, dshift_ref):
    step = pl.program_id(0)
    lanes = q_ref.shape[1]
    means = mean_matrix(lanes, size)
    gain, shift = gain_ref[...], shift_ref[...]
    gain2 = gain * gain
    q, k = q_ref[...], k_ref[...]
    dmix = dmix_ref[...].astype(F32)
    fin = fin_ref[...]
    dfin = dmix * gain
    do = inv_ref[...] * (dfin - head_mean(dfin, means) - fin * head_mean(dfin * fin, means))
    do_ref[...] = do

    @pl.when(step == 0)
    def _():
        dgain_ref[...] = jnp.zeros_like(dgain_ref)
        dshift_ref[...] = jnp.zeros_like(dshift_ref)

    dgain_ref[...] += jnp.sum(dmix * fin, axis=0, keepdims=True)
    dshift_ref[...] += jnp.sum(dmix, axis=0, keepdims=True)
    gr = (rate_ref[...] * g_ref[...])
    w = w_ref[...]
    at = [lax.broadcasted_iota(jnp.int32, w.shape, d) // MB for d in range(2)]
    w_in = jnp.where(at[0] == at[1], w, 0.0)
    do_b = do.astype(BF)
    dq = dmix + dot_nt(do_b, wz_ref[...].astype(BF)) + jnp.where(seg_ref[...] == seg_before_ref[step], dot_nt(do_b, s_ref[0].astype(BF)), 0.0)
    gr_b = gr.astype(BF)
    dgo = jnp.zeros_like(do)
    do_hi, do_lo = split(do)
    for mine in head_masks(q.shape, size):
        da = w * dot_nt(only(mine, do_b), gr_b)
        dq -= dot(da.astype(BF), only(mine, k))
        a = w_in * (dot_nt(only(mine, q), k) + 1.0)
        a_hi, a_lo = split(a)
        dh, dl = only(mine, do_hi), only(mine, do_lo)
        dgo -= dot_tn(a_hi, dh) + dot_tn(a_lo, dh) + dot_tn(a_hi, dl)
    dq_ref[...] = dq.astype(BF)
    dgo_ref[...] = dgo
    z = z_ref[...]
    s = lax.rsqrt(head_mean(z * z, means) + EPS)
    n = z * s
    d = shift - (v_ref[...].astype(F32) - k.astype(F32))
    gs = gain * (gain * n + d)
    m2 = head_mean(gs * n, means)
    p = gs + gain2 * n
    k1, k2 = head_mean(p, means), head_mean(p * n, means) + 2.0 * m2
    ss = s * s
    alpha_ref[...] = ss * (gain2 - m2)
    p_ref[...] = p
    p2_ref[...] = ss * (p - k1 - k2 * n)
    n_ref[...] = n
    n2_ref[...] = ss * n
    sn_ref[...] = s


def out_bwd(seg_before, dmix, q, k, v, z, g, rate, seg, w, states, fin, inv, wz, gain, shift, size):
    tokens, lanes = q.shape
    rows = rows_spec(lanes)
    full = jax.ShapeDtypeStruct((tokens, lanes), F32)
    row = jax.ShapeDtypeStruct((1, lanes), F32)
    return pl.pallas_call(
        functools.partial(out_bwd_kernel, size),
        grid=(tokens // BLK,),
        out_shape=(jax.ShapeDtypeStruct((tokens, lanes), BF),) + (full,) * 8 + (row,) * 2,
        in_specs=[smem()] + [rows] * 8 + [rows_spec(BLK), state_spec(lanes, lanes), rows, rows,
                                          whole(lanes, lanes), whole(1, lanes), whole(1, lanes)],
        out_specs=(rows,) * 9 + (whole(1, lanes),) * 2,
        name="out_bwd",
    )(seg_before, dmix, q, k, v, z, g, rate, seg, w, states, fin, inv, wz, gain, shift)


def scan_bwd_kernel(size, mean_of, steps_ref, table_ref, last_ref, q_ref, k_ref, seg_ref, rate_ref, gain_ref, do_ref, dgo_ref, alpha_ref, p_ref, p2_ref, n_ref, n2_ref, sn_ref,
                    dz_ref, dg_ref, d_ref, db_ref, dzb_ref, dgb_ref, sw_ref, s2_ref, bw_ref):
    tokens, lanes = k_ref.shape
    mask = head_blocks(lanes, size)
    gain2 = gain_ref[...] * gain_ref[...]
    sw_ref[...] = jnp.zeros_like(sw_ref)
    s2_ref[...] = jnp.zeros_like(s2_ref)
    bw_ref[...] = jnp.zeros_like(bw_ref)

    def step(t, carry):
        for lane in range(2):
            m, write, slot = table_ref[lane, 0, t], table_ref[lane, 1, t], table_ref[lane, 2, t]
            rows = pl.ds(pl.multiple_of(m * MB, MB), MB)
            to = pl.ds(pl.multiple_of(write * MB, MB), MB)
            last_before, last_here = last_ref[m], last_ref[m + 1]
            q, k = q_ref[rows, :], k_ref[rows, :]
            seg = seg_ref[rows, :]
            state = sw_ref[lane]
            d_ref[slot] = state
            db_ref[slot] = bw_ref[lane]
            y = dot(jnp.concatenate([k, k], axis=1), s2_ref[lane]) + bw_ref[lane, 0:1, :]
            dg = dgo_ref[rows, :] - jnp.where(seg == last_here, y, 0.0) * (1.0 / MB)
            u = rate_ref[rows, :] * dg
            p, n = p_ref[rows, :], n_ref[rows, :]
            r1, r2, rp = mean_of(u * n), mean_of(u * gain2), mean_of(u * p)
            dz = alpha_ref[rows, :] * u - p2_ref[rows, :] * r1 - n2_ref[rows, :] * rp - sn_ref[rows, :] * (sn_ref[rows, :] * r2)
            dzb_ref[to, :] = dz
            dgb_ref[to, :] = dg
            goes = seg == last_before
            dz_c, do_c = jnp.where(goes, dz, 0.0), jnp.where(goes, do_ref[rows, :], 0.0)
            z_hi, z_lo = split(dz_c)
            o_hi, o_lo = split(do_c)
            delta = dot_tn(jnp.concatenate([k, k], axis=0), jnp.concatenate([z_hi, z_lo], axis=0))
            delta += dot_tn(jnp.concatenate([q, q], axis=0), jnp.concatenate([o_hi, o_lo], axis=0))
            keep = jnp.where(last_before == last_here, 1.0, 0.0)
            state = keep * state + jnp.where(mask, delta, 0.0)
            sw_ref[lane] = state
            s_hi, s_lo = split(state)
            s2_ref[lane] = jnp.concatenate([s_hi, s_lo], axis=0)
            bw_ref[lane] = keep * bw_ref[lane] + jnp.sum(dz_c + do_c, axis=0, keepdims=True)
        return carry

    lax.fori_loop(0, steps_ref[0], step, 0)
    dz_ref[...] = dzb_ref[0:tokens, :]
    dg_ref[...] = dgb_ref[0:tokens, :]


def scan_bwd(schedule, q, k, seg, rate, gain, parts, size, mean_of):
    steps, _, table, last = schedule
    tokens, lanes = k.shape
    blocks = tokens // BLK
    return pl.pallas_call(
        functools.partial(scan_bwd_kernel, size, mean_of),
        out_shape=(
            jax.ShapeDtypeStruct((tokens, lanes), F32),
            jax.ShapeDtypeStruct((tokens, lanes), F32),
            jax.ShapeDtypeStruct((blocks + 1, lanes, lanes), F32),
            jax.ShapeDtypeStruct((blocks + 1, 8, lanes), F32),
        ),
        in_specs=[smem()] * 3 + [vmem()] * 13,
        out_specs=(vmem(),) * 4,
        scratch_shapes=[
            pltpu.VMEM((tokens + MB, lanes), F32),
            pltpu.VMEM((tokens + MB, lanes), F32),
            pltpu.VMEM((2, lanes, lanes), F32),
            pltpu.VMEM((2, 2 * lanes, lanes), BF),
            pltpu.VMEM((2, 8, lanes), F32),
        ],
        compiler_params=pltpu.CompilerParams(vmem_limit_bytes=60 * 1024 * 1024),
        name="scan_bwd",
    )(steps, table, last, q, k, seg, rate, gain, *parts)


def post_bwd_kernel(size, seg_before_ref, q_ref, k_ref, v_ref, g_ref, rate_ref, seg_ref, w_ref, s_ref, d_ref, n_ref, sn_ref, do_ref, dz_ref, dg_ref, wz_ref, gain_ref, shift_ref,
                    dk_ref, dv_ref, dl_ref, dwz_ref, dbz_ref, dgain_ref, dshift_ref, drb_ref):
    step = pl.program_id(0)
    lanes = q_ref.shape[1]
    means = mean_matrix(lanes, size)
    gain, shift = gain_ref[...], shift_ref[...]
    q, k = q_ref[...], k_ref[...]
    rate, g, n, s = rate_ref[...], g_ref[...], n_ref[...], sn_ref[...]
    do, dz, dg = do_ref[...], dz_ref[...], dg_ref[...]
    seg = seg_ref[...]

    @pl.when(step == 0)
    def _():
        for ref in (dwz_ref, dbz_ref, dgain_ref, dshift_ref, drb_ref):
            ref[...] = jnp.zeros_like(ref)

    u = rate * dg
    dgs = s * (u - n * head_mean(u * n, means))
    de = gain * dgs
    e = gain * n + shift - (v_ref[...].astype(F32) - k.astype(F32))
    dv_ref[...] = (-de).astype(BF)
    gr = (rate * g).astype(BF)
    w = w_ref[...]
    at = [lax.broadcasted_iota(jnp.int32, w.shape, d) // MB for d in range(2)]
    w_out = jnp.where(at[0] > at[1], w, 0.0)
    do_b, dz_b = do.astype(BF), dz.astype(BF)
    dk = de + dot_nt(dz_b, wz_ref[...].astype(BF)) + jnp.where(seg == seg_before_ref[step], dot_nt(dz_b, s_ref[0].astype(BF)), 0.0)
    dk -= jnp.where(seg == seg_before_ref[step + 1], dot_nt(gr, d_ref[0].astype(BF)), 0.0) * (1.0 / MB)
    for mine in head_masks(q.shape, size):
        do_g = (w * dot_nt(only(mine, do_b), gr)).astype(BF)
        dz_g = (w_out * dot_nt(only(mine, dz_b), gr)).astype(BF)
        kh = only(mine, k)
        dk -= dot(dz_g, kh) + dot_tn(dz_g, kh) + dot_tn(do_g, only(mine, q))
    dk_ref[...] = dk.astype(BF)
    drate = head_mean(g * dg, means) * size
    dl = drate * rate * (1.0 - size * rate)
    dl_ref[...] = dl
    drb_ref[...] += jnp.sum(dl, axis=0, keepdims=True)
    dz_lo = (dz - dz_b.astype(F32)).astype(BF)
    do_lo = (do - do_b.astype(F32)).astype(BF)
    dwz_ref[...] += dot_tn(q, do_b) + dot_tn(k, dz_b) + dot_tn(q, do_lo) + dot_tn(k, dz_lo)
    dbz_ref[...] += jnp.sum(do + dz, axis=0, keepdims=True)
    dgain_ref[...] += jnp.sum(dgs * e + de * n, axis=0, keepdims=True)
    dshift_ref[...] += jnp.sum(de, axis=0, keepdims=True)


def post_bwd(seg_before, q, k, v, g, rate, seg, w, states, d_states, n, sn, do, dz, dg, wz, gain, shift, size):
    tokens, lanes = q.shape
    rows = rows_spec(lanes)
    row = jax.ShapeDtypeStruct((1, lanes), F32)
    half = jax.ShapeDtypeStruct((tokens, lanes), BF)
    return pl.pallas_call(
        functools.partial(post_bwd_kernel, size),
        grid=(tokens // BLK,),
        out_shape=(half, half, jax.ShapeDtypeStruct((tokens, lanes), F32), jax.ShapeDtypeStruct((lanes, lanes), F32), row, row, row, row),
        in_specs=[smem()] + [rows] * 6 + [rows_spec(BLK)] + [state_spec(lanes, lanes)] * 2 + [rows] * 5
        + [whole(lanes, lanes), whole(1, lanes), whole(1, lanes)],
        out_specs=(rows,) * 3 + (whole(lanes, lanes),) + (whole(1, lanes),) * 4,
        name="post_bwd",
    )(seg_before, q, k, v, g, rate, seg, w, states, d_states, n, sn, do, dz, dg, wz, gain, shift)


def prepare(segments, logits, state_init, offset_init, inner_gain, inner_shift, rate_bias):
    heads, size = offset_init.shape
    lanes = heads * size
    centred = state_init - jnp.mean(state_init, axis=-1, keepdims=True)
    wz = jnp.zeros((lanes, lanes), F32)
    for h in range(heads):
        wz = wz.at[h * size:(h + 1) * size, h * size:(h + 1) * size].set(centred[h])
    bz = (offset_init - jnp.mean(offset_init, axis=-1, keepdims=True)).reshape(1, lanes)
    rate = jnp.repeat(jax.nn.sigmoid(logits.astype(F32) + rate_bias[None, :]) / size, size, axis=1)
    seg = jnp.broadcast_to(segments[:, None], (segments.shape[0], lanes))
    seg_before = jnp.concatenate([jnp.full((1,), -1, jnp.int32), segments[BLK - 1::BLK]])
    return dict(wz=wz, bz=bz, rate=rate, seg=seg, seg_before=seg_before, w=weights_of(segments), schedule=lane_schedule(segments),
                gain=inner_gain.reshape(1, lanes), shift=inner_shift.reshape(1, lanes), size=size)


def mixer_fwd(c, q, k, v):
    mean_of = functools.partial(lane_mean, size=c["size"])
    z, g, states, biases = scan_fwd(c["schedule"], k, v, c["seg"], c["rate"], c["wz"], c["bz"], c["gain"], c["shift"], c["size"], mean_of)
    mixed, fin, inv = out_fwd(c["seg_before"], q, k, g, c["rate"], c["seg"], c["w"], states, biases, c["wz"], c["bz"], c["gain"], c["shift"], c["size"])
    return mixed, (q, k, v, z, g, states, fin, inv)


def mixer_bwd(c, kept, dmix):
    mean_of = functools.partial(lane_mean, size=c["size"])
    q, k, v, z, g, states, fin, inv = kept
    size = c["size"]
    dq, do, dgo, alpha, p, p2, n, n2, sn, dgain, dshift = out_bwd(
        c["seg_before"], dmix, q, k, v, z, g, c["rate"], c["seg"], c["w"], states, fin, inv, c["wz"], c["gain"], c["shift"], size)
    dz, dg, d_states, _ = scan_bwd(c["schedule"], q, k, c["seg"], c["rate"], c["gain"], (do, dgo, alpha, p, p2, n, n2, sn), size, mean_of)
    dk, dv, dl, dwz, dbz, dgain2, dshift2, drb = post_bwd(
        c["seg_before"], q, k, v, g, c["rate"], c["seg"], c["w"], states, d_states, n, sn, do, dz, dg, c["wz"], c["gain"], c["shift"], size)
    heads = q.shape[1] // size
    dstate = jnp.stack([dwz[h * size:(h + 1) * size, h * size:(h + 1) * size] for h in range(heads)])
    by_head = lambda row: row.reshape(heads, size)
    return (dq, dk, dv, dl[:, ::size].astype(BF), dstate, by_head(dbz), by_head(dgain + dgain2), by_head(dshift + dshift2), drb.reshape(heads, size)[:, 0])


def rms_piece(values, gain):
    return values * lax.rsqrt(jnp.mean(values * values, axis=-1, keepdims=True) + EPS) * gain


def gelu_piece(values):
    return jax.nn.gelu(values, approximate=True)


def product(left, right):
    return jnp.dot(left, right, preferred_element_type=F32)


def outer_sum(left, right):
    return lax.dot_general(left, right, (((0,), (0,)), ((), ())), preferred_element_type=F32)


def back_product(left, right):
    return lax.dot_general(left, right, (((1,), (1,)), ((), ())), preferred_element_type=F32)


def swap(values, axis, mask):
    return lax.ppermute(values, axis, [(i, i ^ mask) for i in range(lax.axis_size(axis))])


def halving_orders():
    rows = [("row", 1 << i) for i in range(lax.axis_size("row").bit_length() - 1)]
    seqs = [("seq", 1 << i) for i in range(lax.axis_size("seq").bit_length() - 1)]
    core, xs = rows[:1], rows[1:]
    cut = len(seqs) // 2
    ys, zs = seqs[:cut], seqs[cut:]
    return (core + xs + ys + zs, core + ys + zs[:1] + xs + zs[1:], core + zs[:1] + xs + ys + zs[1:])


def relative_order(order, features):
    blocks = 1 << len(order)
    at = np.arange(features) // (features // blocks)
    flips = {"row": np.zeros(features, np.int32), "seq": np.zeros(features, np.int32)}
    for i, (axis, mask) in enumerate(order):
        flips[axis] += ((at >> (len(order) - 1 - i)) & 1) * mask
    block = (lax.axis_index("row") ^ flips["row"]) * lax.axis_size("seq") + (lax.axis_index("seq") ^ flips["seq"])
    source = block * (features // blocks) + np.arange(features) % (features // blocks)
    return (jnp.arange(features)[:, None] == source[None, :]).astype(BF)


def reduce_outer(left, right, order):
    half = left.shape[1] // 2
    send = outer_sum(left[:, half:], right).astype(BF)
    keep = outer_sum(left[:, :half], right).astype(BF)
    for axis, mask in order[:-1]:
        got = swap(send, axis, mask)
        half = half // 2
        send = (keep[half:].astype(F32) + got[half:].astype(F32)).astype(BF)
        keep = (keep[:half].astype(F32) + got[:half].astype(F32)).astype(BF)
    axis, mask = order[-1]
    return keep.astype(F32) + swap(send, axis, mask).astype(F32)


def shards(
    tokens_in, segment_ids, norm_in_gain, query_weight, key_weight, value_weight, rate_weight, gate_weight, out_weight,
    state_init, offset_init, inner_gain, inner_shift, rate_bias, norm_post_gain, norm_mlp_gain, ffn_gate, ffn_up, ffn_down, cotangent,
):
    row_count, token_count, features = tokens_in.shape
    assert row_count == 1
    groups = lax.axis_size("seq")
    heads_here, size = offset_init.shape
    lanes = heads_here * size
    flat_in = tokens_in[0].astype(F32)
    normed_f, norm_in_pull = jax.vjp(rms_piece, flat_in, norm_in_gain)
    normed_in = normed_f.astype(BF)

    def to_heads(values):
        width = values.shape[1] // groups
        split_up = jnp.swapaxes(values.astype(BF).reshape(token_count, groups, width), 0, 1)
        return lax.all_to_all(split_up, "seq", split_axis=0, concat_axis=0, tiled=True).reshape(groups * token_count, width)

    def to_tokens(values):
        width = values.shape[1]
        moved = lax.all_to_all(values.reshape(groups, token_count, width), "seq", split_axis=0, concat_axis=0, tiled=True)
        return jnp.swapaxes(moved, 0, 1).reshape(token_count, groups * width)

    k_heads = to_heads(product(normed_in, key_weight))
    v_heads = to_heads(product(normed_in, value_weight))
    r_heads = to_heads(product(normed_in, rate_weight))
    q_heads = to_heads(product(normed_in, query_weight))
    parts = prepare(segment_ids[0], r_heads, state_init, offset_init, inner_gain, inner_shift, rate_bias)
    mixed_heads, kept = mixer_fwd(parts, q_heads, k_heads, v_heads)
    mixed_f = to_tokens(mixed_heads).astype(F32)
    post_norm, post_pull = jax.vjp(rms_piece, mixed_f, norm_post_gain)
    gate_pre = product(normed_in, gate_weight)
    gelu_out, gelu_pull = jax.vjp(gelu_piece, gate_pre)
    branch = (post_norm * gelu_out).astype(BF)
    middle = flat_in + product(branch, out_weight)
    normed_mid_f, mid_pull = jax.vjp(rms_piece, middle, norm_mlp_gain)
    normed_mid = normed_mid_f.astype(BF)
    gate_proj = product(normed_mid, ffn_gate)
    up_proj = product(normed_mid, ffn_up)
    silu_out, silu_pull = jax.vjp(jax.nn.silu, gate_proj)
    hidden = (silu_out * up_proj).astype(BF)
    block_out = (middle + product(hidden, ffn_down)).astype(BF)
    grad_ffn = cotangent[0]
    grad_out = grad_ffn.astype(F32)
    order_a, order_b, order_c = halving_orders()
    rel_a, rel_b, rel_c = [relative_order(order, features) for order in (order_a, order_b, order_c)]

    def put(values, rel):
        return product(values, rel).astype(BF)

    grad_down = reduce_outer(put(grad_ffn, rel_a), hidden, order_a).T
    grad_hidden = back_product(grad_ffn, ffn_down)
    grad_gate_proj = silu_pull(grad_hidden * up_proj)[0].astype(BF)
    grad_up_proj = (grad_hidden * silu_out).astype(BF)
    grad_ffn_gate = reduce_outer(put(normed_mid, rel_b), grad_gate_proj, order_b)
    grad_ffn_up = reduce_outer(put(normed_mid, rel_c), grad_up_proj, order_c)
    grad_normed_mid = back_product(grad_gate_proj, ffn_gate) + back_product(grad_up_proj, ffn_up)
    grad_mid_part, grad_norm_mlp = mid_pull(grad_normed_mid)
    grad_middle = grad_out + grad_mid_part
    grad_branch_out = grad_middle.astype(BF)
    grad_out_proj = reduce_outer(put(branch, rel_a), grad_branch_out, order_a)
    grad_branch = back_product(grad_branch_out, out_weight)
    grad_gate_pre = gelu_pull(grad_branch * post_norm)[0].astype(BF)
    in_a, in_b, in_c = put(normed_in, rel_a), put(normed_in, rel_b), put(normed_in, rel_c)
    grad_gate = reduce_outer(in_b, grad_gate_pre, order_b)
    grad_mixed_part, grad_norm_post = post_pull(grad_branch * gelu_out)
    grad_heads = to_heads(grad_mixed_part)
    grad_q, grad_k, grad_v, grad_r, grad_state, grad_offset, grad_igain, grad_ishift, grad_rbias = mixer_bwd(parts, kept, grad_heads)
    grad_q_flat = to_tokens(grad_q)
    grad_query = reduce_outer(in_c, grad_q_flat, order_c)
    grad_k_flat = to_tokens(grad_k)
    grad_v_flat = to_tokens(grad_v)
    grad_r_flat = to_tokens(grad_r)
    grad_key = reduce_outer(in_a, grad_k_flat, order_a)
    grad_value_rate = reduce_outer(in_b, jnp.concatenate([grad_v_flat, grad_r_flat], axis=1), order_b)
    grad_value, grad_rate = grad_value_rate[:, :features], grad_value_rate[:, features:]
    by_head = jnp.concatenate(
        [grad_state.reshape(heads_here, -1), grad_offset, grad_igain, grad_ishift, jnp.broadcast_to(grad_rbias[:, None], (heads_here, size))], axis=1
    ).reshape(-1, lanes)
    mask = 1
    while mask < lax.axis_size("row"):
        by_head = by_head + swap(by_head, "row", mask)
        mask *= 2
    by_head = by_head.reshape(heads_here, -1)
    cuts = [size * size + i * size for i in range(4)]
    grad_normed_in = (
        back_product(grad_q_flat, query_weight)
        + back_product(grad_k_flat, key_weight)
        + back_product(grad_v_flat, value_weight)
        + back_product(grad_r_flat, rate_weight)
        + back_product(grad_gate_pre, gate_weight)
    )
    grad_in_part, grad_norm_in = norm_in_pull(grad_normed_in)
    grad_tokens = grad_middle + grad_in_part
    devices = groups * lax.axis_size("row")
    gains = jnp.stack([grad_norm_in, grad_norm_post, grad_norm_mlp]).reshape(3, devices, features // devices)
    gains = jnp.swapaxes(gains, 0, 1).reshape(devices, -1)
    gains = jnp.sum(lax.all_to_all(gains, ("row", "seq"), split_axis=0, concat_axis=0, tiled=True), axis=0).reshape(3, -1)
    return (
        block_out[None], grad_tokens[None], gains[0], grad_query, grad_key, grad_value, grad_rate, grad_gate, grad_out_proj,
        by_head[:, :cuts[0]].reshape(heads_here, size, size), by_head[:, cuts[0]:cuts[1]], by_head[:, cuts[1]:cuts[2]],
        by_head[:, cuts[2]:cuts[3]], by_head[:, cuts[3]], gains[1], gains[2], grad_ffn_gate, grad_ffn_up, grad_down,
    )


def solution(mesh):
    whole_copy, tokens, heads = P(), P("row", "seq", None), P("seq")
    both = P(("row", "seq"))
    return jax.shard_map(
        shards,
        mesh=mesh,
        in_specs=(tokens, P("row", None)) + (whole_copy,) * 7 + (heads,) * 5 + (whole_copy,) * 5 + (tokens,),
        out_specs=(tokens, tokens) + (both,) * 7 + (heads,) * 5 + (both,) * 4 + (P(None, ("row", "seq")),),
        check_vma=False,
    )
```

time: 3560 us -> 630 us (0.18)
  waiting for transfers between devices: 1380 us -> 105 us
  matrix products: 1060 us -> 83.8 us
  other arithmetic: 477 us -> 78.4 us
  local copies, waits for them, and re-layouts: 414 us -> 119 us
  blocking collectives: 133 us -> 0 us
  Pallas kernels: 0 us -> 130 us
  starting transfers between devices: 30.3 us -> 96.5 us
    reduce_scatter x8 -> x0, waiting for transfers between devices: 1370 us -> none  [the longest x1 252 us: shards(): lax.psum_scatter(grad_ffn_up, ('row', 'seq'), scatter_dimension=0, tiled=...]
    dot_general x3945 -> x16, matrix products: 1010 us -> 30.3 us  [product(): return jnp.dot(left, right, preferred_element_type=F32)]
    reduce_sum x1233 -> x3, other arithmetic: 201 us -> 0.26 us  [the longest x1 0.12 us: prepare(): jnp.mean(offset_init, axis=-1, keepdims=True)]
    squeeze x192 -> x0, local copies, waits for them, and re-layouts: 154 us -> none  [inner_loop(): lax.scan(stepper, initial, (blocked(queries), blocked(keys_in), blocked(v...]
    pallas_call x0 -> x5, Pallas kernels: none -> 130 us  [the longest x1 46.1 us: scan_fwd(): pl.pallas_call(functools.partial(scan_fwd_kernel, size, mean_of), out_sha...]
    unnamed x19 -> x4, other arithmetic: 86.7 us -> 2.01 us
    all_to_all x5 -> x0, blocking collectives: 80.5 us -> none  [the longest x1 18.5 us: shards(): lax.all_to_all(to_tokens(mixed_heads), 'seq', split_axis=1, concat_axis=2...]
    ppermute x0 -> x42, waiting for transfers between devices: none -> 74.5 us  [swap(): lax.ppermute(values, axis, [(i, i ^ mask) for i in range(lax.axis_size(ax...]
where the time goes in v1:
time: 630 us; the launch traced here: 619 us
  Pallas kernels  130 us (21%)
  local copies, waits for them, and re-layouts  119 us (19%)
  waiting for transfers between devices  105 us (17%)
  starting transfers between devices  96.5 us (15%)
  matrix products  83.8 us (13%)
  other arithmetic  78.4 us (12%)
    ppermute x42, waiting for transfers between devices, swap(): lax.ppermute(values, axis, [(i, i ^ mask) for i in range(lax.axis_size(ax...  74.5 us
    convert_element_type x24, other arithmetic, reduce_outer(): keep = (keep[:half].astype(F32) + got[:half].astype(F32)).astype(BF)  51.4 us
    pallas_call x1, Pallas kernels, scan_fwd(): pl.pallas_call(functools.partial(scan_fwd_kernel, size, mean_of), out_sha...  46.1 us
    unnamed x183, local copies, waits for them, and re-layouts  44.2 us
    ppermute x42, starting transfers between devices, swap(): lax.ppermute(values, axis, [(i, i ^ mask) for i in range(lax.axis_size(ax...  44.1 us
    dot_general x16, matrix products, outer_sum(): lax.dot_general(left, right, (((0,), (0,)), ((), ())), preferred_element_...  36.1 us
    pallas_call x1, Pallas kernels, scan_bwd(): pl.pallas_call(functools.partial(scan_bwd_kernel, size, mean_of), out_sha...  32.8 us
    dot_general x16, matrix products, product(): return jnp.dot(left, right, preferred_element_type=F32)  30.3 us
  transfers between devices with their start and end apart: 53, of which 22 were waited for; matrix products, arithmetic and copies ran while one was open for 38% of the time, Pallas kernels for 18%

profile of v1, /device:TPU:0, one launch (start us, length us, event | category | flops | bytes accessed | tf_op | source)
XLA Modules:
  0.0 618.6 jit_solution(13497664148964693244)
XLA Ops:
  4.6 7.3 %all-to-all-start.3 = ((bf16[8,256,2]{1,2,0:T(2,128)(2,1)}), bf16[8,256,2]{1,2,0:T(2,128)(2,1)S(1)}, u32[]{:S(2)}, u32[]{:S(2)}) async-start(bf16[8,256,2]{1,2,0:T(2,128)(2,1)} %bitcast.13), calls=%async_computation.3 | async-start | bytes 16384 | tf_op jit(solution)/shard_map/all_to_all | solution.py:591
  17.2 3.5 fusion.34
  24.9 6.0 all-to-all-start.1
  31.1 3.1 fusion.33
  34.2 10.7 %all-to-all-done.1 = bf16[8,256,128]{2,1,0:T(8,128)(2,1)S(1)} async-done(((bf16[8,256,128]{2,1,0:T(8,128)(2,1)}), bf16[8,256,128]{2,1,0:T(8,128)(2,1)S(1)}, u32[]{:S(2)}, u32[]{:S(2)}) %all-to-all-start.1) | async-done | bytes 524320 | tf_op jit(solution)/shard_map/all_to_all | solution.py:591
  45.0 3.8 all-to-all-start.2
  56.0 7.0 %all-to-all-done.2 = bf16[8,256,128]{2,1,0:T(8,128)(2,1)S(1)} async-done(((bf16[8,256,128]{2,1,0:T(8,128)(2,1)}), bf16[8,256,128]{2,1,0:T(8,128)(2,1)S(1)}, u32[]{:S(2)}, u32[]{:S(2)}) %all-to-all-start.2) | async-done | bytes 524320 | tf_op jit(solution)/shard_map/all_to_all | solution.py:591
  63.8 3.6 all-to-all-start
  75.1 46.1 %scan_fwd.1 = (f32[2048,128]{1,0:T(8,128)}, f32[2048,128]{1,0:T(8,128)}, f32[17,128,128]{2,1,0:T(8,128)}, f32[17,8,128]{2,1,0:T(8,128)}) custom-call(s32[1]{0:T(128)} %bitcast.8.steps_ref, s32[2,3,130]{2,1,0:T(4,128)} %pad_add_fusion.table_ref, s32[129]{0:T(256)} %pad_add_fusion.3.last_ref, bf16[2048,128]{1,0:T(8,128)(2,1)} %bitcast.192, ...), custom_call_target="tpu_custom_call" | custom-call | tf_op jit(solution)/shard_map/scan_fwd/pallas_call | solution.py:169
  122.0 15.9 %out_fwd.1 = (bf16[2048,128]{1,0:T(8,128)(2,1)}, f32[2048,128]{1,0:T(8,128)}, f32[2048,128]{1,0:T(8,128)}) custom-call(s32[17]{0:T(128)} %pad_add_fusion.4.seg_before_ref, bf16[2048,128]{1,0:T(8,128)(2,1)} %bitcast.197, bf16[2048,128]{1,0:T(8,128)(2,1)} %bitcast.193, f32[2048,128]{1,0:T(8,128)} %get-tuple-element.74.g_ref, f32[2048,128]{1,0:T(8,128)} %copy.135.rate_ref, ...), custom_call_target="tpu_custom_call" | custom-call | tf_op jit(solution)/shard_map/out_fwd/pallas_call | solution.py:259
  137.9 6.2 %all-to-all-start.4 = ((bf16[8,256,128]{2,1,0:T(8,128)(2,1)}), bf16[8,256,128]{2,1,0:T(8,128)(2,1)S(1)}, u32[]{:S(2)}, u32[]{:S(2)}) async-start(bf16[8,256,128]{2,1,0:T(8,128)(2,1)} %bitcast.222), calls=%async_computation.4 | async-start | bytes 1048576 | tf_op jit(solution)/shard_map/all_to_all | solution.py:595
  150.4 7.7 %all-to-all-done.4 = bf16[8,256,128]{2,1,0:T(8,128)(2,1)S(1)} async-done(((bf16[8,256,128]{2,1,0:T(8,128)(2,1)}), bf16[8,256,128]{2,1,0:T(8,128)(2,1)S(1)}, u32[]{:S(2)}, u32[]{:S(2)}) %all-to-all-start.4) | async-done | bytes 524320 | tf_op jit(solution)/shard_map/all_to_all | solution.py:595
  165.8 3.3 multiply_convert_fusion
  196.2 4.1 all-to-all-start.5
  203.5 3.7 convolution_convert_fusion.1
  207.2 5.1 fusion.39
  214.2 18.7 %out_bwd.1 = (bf16[2048,128]{1,0:T(8,128)(2,1)}, f32[2048,128]{1,0:T(8,128)}, f32[2048,128]{1,0:T(8,128)}, f32[2048,128]{1,0:T(8,128)}, f32[2048,128]{1,0:T(8,12...) custom-call(s32[17]{0:T(128)} %pad_add_fusion.4.seg_before_ref, ...), custom_call_target="tpu_custom_call" | custom-call | tf_op jit(solution)/shard_map/out_bwd/pallas_call | solution.py:335
  232.9 32.8 %scan_bwd.1 = (f32[2048,128]{1,0:T(8,128)}, f32[2048,128]{1,0:T(8,128)}, f32[17,128,128]{2,1,0:T(8,128)}, f32[17,8,128]{2,1,0:T(8,128)}) custom-call(s32[1]{0:T(128)} %bitcast.8.steps_ref, s32[2,3,130]{2,1,0:T(4,128)} %pad_add_fusion.1.table_ref, s32[129]{0:T(256)} %pad_add_fusion.3.last_ref, bf16[2048,128]{1,0:T(8,128)(2,1)} %bitcast.199, ...), custom_call_target="tpu_custom_call" | custom-call | tf_op jit(solution)/shard_map/scan_bwd/pallas_call | solution.py:397
  265.7 16.5 %post_bwd.1 = (bf16[2048,128]{1,0:T(8,128)(2,1)}, bf16[2048,128]{1,0:T(8,128)(2,1)}, f32[2048,128]{1,0:T(8,128)}, f32[128,128]{1,0:T(8,128)}, f32[1,128]{1,0:T(1...) custom-call(s32[17]{0:T(128)} %pad_add_fusion.4.seg_before_ref, bf16[2048,128]{1,0:T(8,128)(2,1)} %bitcast.200, ...), custom_call_target="tpu_custom_call" | custom-call | tf_op jit(solution)/shard_map/post_bwd/pallas_call | solution.py:470
  284.7 3.9 slice.539
  290.5 3.9 all-to-all-start.9
  300.9 3.8 all-to-all-start.8
  311.1 2.9 add_convert_fusion.15
  314.5 2.6 add_convert_fusion.17
  320.0 4.5 all-to-all-start.6
  340.9 5.5 all-to-all-start.7
  359.2 2.8 convolution_add_fusion.2
  366.3 3.6 all-to-all-start.10
  383.1 2.6 collective-permute-start.24
  386.6 3.2 collective-permute-done.24
  392.6 3.7 collective-permute-done.19
  398.4 3.5 fusion.108
  406.1 4.5 add_convert_fusion.1
  414.6 3.1 fusion.109
  421.9 4.4 add_convert_fusion.3
  429.0 3.5 fusion.110
  437.6 3.1 add_convert_fusion.19
  441.2 2.7 add_convert_fusion.21
  452.2 2.8 copy.150
  460.1 12.7 %collective-permute-done.1 = bf16[256,1024]{1,0:T(8,128)(2,1)} collective-permute-done((bf16[256,1024]{1,0:T(8,128)(2,1)}, bf16[256,1024]{1,0:T(8,128)(2,1)}, u32[]{:S(2)}, u32[]{:S(2)}) %collective-permute-start.1) | collective-permute-done | bytes 524320 | tf_op jit(solution)/shard_map/ppermute | solution.py:539
  477.5 19.7 %collective-permute-done.7 = bf16[128,1024]{1,0:T(8,128)(2,1)S(1)} collective-permute-done((bf16[128,1024]{1,0:T(8,128)(2,1)S(1)}, bf16[128,1024]{1,0:T(8,128)(2,1)S(1)}, u32[]{:S(2)}, u32[]{:S(2)}) %collective-permute-start.7) | collective-permute-done | bytes 262176 | tf_op jit(solution)/shard_map/ppermute | solution.py:539
  499.4 5.5 collective-permute-done.12
  514.9 5.1 collective-permute-done.9
  522.1 7.2 %collective-permute-done.14 = bf16[32,1040]{0,1:T(8,128)(2,1)S(1)} collective-permute-done((bf16[32,1040]{0,1:T(8,128)(2,1)S(1)}, bf16[32,1040]{0,1:T(8,128)(2,1)S(1)}, u32[]{:S(2)}, u32[]{:S(2)}) %collective-permute-start.14) | collective-permute-done | bytes 66592 | tf_op jit(solution)/shard_map/ppermute | solution.py:539
  539.9 3.3 add_convert_fusion.7
  554.0 2.8 add_convert_fusion.9
  567.6 2.8 add_convert_fusion.11
  605.5 7.4 %collective-permute-done.41 = bf16[32,2736]{1,0:T(8,128)(2,1)S(1)} collective-permute-done((bf16[32,2736]{1,0:T(8,128)(2,1)S(1)}, bf16[32,2736]{1,0:T(8,128)(2,1)S(1)}, u32[]{:S(2)}, u32[]{:S(2)}) %collective-permute-start.41) | collective-permute-done | bytes 175136 | tf_op jit(solution)/shard_map/ppermute | solution.py:539
  (450 shorter events, 271.3 us)
Async XLA Ops:
  4.6 20.3 %all-to-all-start.3 = ((bf16[8,256,2]{1,2,0:T(2,128)(2,1)}), bf16[8,256,2]{1,2,0:T(2,128)(2,1)S(1)}, u32[]{:S(2)}, u32[]{:S(2)}) async-start(bf16[8,256,2]{1,2,0:T(2,128)(2,1)} %bitcast.13), calls=%async_computation.3 | async-start | bytes 16384 | tf_op jit(solution)/shard_map/all_to_all | solution.py:591
  24.9 20.0 %all-to-all-start.1 = ((bf16[8,256,128]{2,1,0:T(8,128)(2,1)}), bf16[8,256,128]{2,1,0:T(8,128)(2,1)S(1)}, u32[]{:S(2)}, u32[]{:S(2)}) async-start(bf16[8,256,128]{2,1,0:T(8,128)(2,1)} %bitcast.216), calls=%async_computation.1 | async-start | bytes 1048576 | tf_op jit(solution)/shard_map/all_to_all | solution.py:591
  45.0 18.0 %all-to-all-start.2 = ((bf16[8,256,128]{2,1,0:T(8,128)(2,1)}), bf16[8,256,128]{2,1,0:T(8,128)(2,1)S(1)}, u32[]{:S(2)}, u32[]{:S(2)}) async-start(bf16[8,256,128]{2,1,0:T(8,128)(2,1)} %bitcast.214), calls=%async_computation.2 | async-start | bytes 1048576 | tf_op jit(solution)/shard_map/all_to_all | solution.py:591
  63.8 57.4 %all-to-all-start = ((bf16[8,256,128]{2,1,0:T(8,128)(2,1)}), bf16[8,256,128]{2,1,0:T(8,128)(2,1)S(1)}, u32[]{:S(2)}, u32[]{:S(2)}) async-start(bf16[8,256,128]{2,1,0:T(8,128)(2,1)} %bitcast.215), calls=%async_computation | async-start | bytes 1048576 | tf_op jit(solution)/shard_map/all_to_all | solution.py:591
  137.9 20.2 %all-to-all-start.4 = ((bf16[8,256,128]{2,1,0:T(8,128)(2,1)}), bf16[8,256,128]{2,1,0:T(8,128)(2,1)S(1)}, u32[]{:S(2)}, u32[]{:S(2)}) async-start(bf16[8,256,128]{2,1,0:T(8,128)(2,1)} %bitcast.222), calls=%async_computation.4 | async-start | bytes 1048576 | tf_op jit(solution)/shard_map/all_to_all | solution.py:595
  196.2 18.1 %all-to-all-start.5 = ((bf16[8,256,128]{2,1,0:T(8,128)(2,1)}), bf16[8,256,128]{2,1,0:T(8,128)(2,1)}, u32[]{:S(2)}, u32[]{:S(2)}) async-start(bf16[8,256,128]{2,1,0:T(8,128)(2,1)} %bitcast.217), calls=%async_computation.5 | async-start | bytes 1048576 | tf_op jit(solution)/shard_map/all_to_all | solution.py:591
  200.3 110.8 %collective-permute-start.20 = (bf16[512,1024]{1,0:T(8,128)(2,1)}, bf16[512,1024]{1,0:T(8,128)(2,1)}, u32[]{:S(2)}, u32[]{:S(2)}) collective-permute-start(bf16[512,1024]{1,0:T(8,128)(2,1)} %convolution_convert_fusion.8), channel_id=1, source_target_pairs={{0,8},{8,0},{16,24},{24,16},{1,9},{9,1},{17,25},{25,17},{2,10},{10... | collective-permute-start | bytes 3145736 | tf_op jit(solution)/shard_map/ppermute | solution.py:539
  203.0 111.6 %collective-permute-start.15 = (bf16[512,1024]{1,0:T(8,128)(2,1)}, bf16[512,1024]{1,0:T(8,128)(2,1)}, u32[]{:S(2)}, u32[]{:S(2)}) collective-permute-start(bf16[512,1024]{1,0:T(8,128)(2,1)} %convolution_convert_fusion.10), channel_id=1, source_target_pairs={{0,8},{8,0},{16,24},{24,16},{1,9},{9,1},{17,25},{25,17},{2,10},{10... | collective-permute-start | bytes 3145736 | tf_op jit(solution)/shard_map/ppermute | solution.py:539
  290.5 10.4 %all-to-all-start.9 = ((bf16[8,256,2]{1,2,0:T(2,128)(2,1)}), bf16[8,256,2]{1,2,0:T(2,128)(2,1)S(1)}, u32[]{:S(2)}, u32[]{:S(2)}) async-start(bf16[8,256,2]{1,2,0:T(2,128)(2,1)} %copy.145), calls=%async_computation.9 | async-start | bytes 16384 | tf_op jit(solution)/shard_map/all_to_all | solution.py:595
  300.9 18.3 %all-to-all-start.8 = ((bf16[8,256,128]{1,2,0:T(8,128)(2,1)}), bf16[8,256,128]{1,2,0:T(8,128)(2,1)S(1)}, u32[]{:S(2)}, u32[]{:S(2)}) async-start(bf16[8,256,128]{1,2,0:T(8,128)(2,1)} %copy.144), calls=%async_computation.8 | async-start | bytes 1048576 | tf_op jit(solution)/shard_map/all_to_all | solution.py:595
  309.5 20.7 %collective-permute-start.26 = (f32[68,128]{1,0:T(8,128)S(1)}, f32[68,128]{1,0:T(8,128)S(1)}, u32[]{:S(2)}, u32[]{:S(2)}) collective-permute-start(f32[68,128]{1,0:T(8,128)S(1)} %add.645), channel_id=1, source_target_pairs={{0,16},{8,24},{16,0},{24,8},{1,17},{9,25},{17,1},{25,9},{2,18},{10... | collective-permute-start | bytes 104456 | tf_op jit(solution)/shard_map/ppermute | solution.py:539
  314.0 16.9 %collective-permute-start.21 = (bf16[256,1024]{1,0:T(8,128)(2,1)}, bf16[256,1024]{1,0:T(8,128)(2,1)}, u32[]{:S(2)}, u32[]{:S(2)}) collective-permute-start(bf16[256,1024]{1,0:T(8,128)(2,1)} %get-tuple-element.224), channel_id=1, source_target_pairs={{0,16},{8,24},{16,0},{24,8},{1,17},{9,25},{17,1},{25,9},{2,18},{10... | collective-permute-start | bytes 1572872 | tf_op jit(solution)/shard_map/ppermute | solution.py:539
  317.2 18.6 %collective-permute-start.16 = (bf16[256,1024]{1,0:T(8,128)(2,1)}, bf16[256,1024]{1,0:T(8,128)(2,1)}, u32[]{:S(2)}, u32[]{:S(2)}) collective-permute-start(bf16[256,1024]{1,0:T(8,128)(2,1)} %get-tuple-element.226), channel_id=1, source_target_pairs={{0,1},{1,0},{2,3},{3,2},{4,5},{5,4},{6,7},{7,6},{8,9},{9,8},{10,11... | collective-permute-start | bytes 1572872 | tf_op jit(solution)/shard_map/ppermute | solution.py:539
  320.0 20.9 %all-to-all-start.6 = ((bf16[8,256,128]{1,2,0:T(8,128)(2,1)}), bf16[8,256,128]{1,2,0:T(8,128)(2,1)S(1)}, u32[]{:S(2)}, u32[]{:S(2)}) async-start(bf16[8,256,128]{1,2,0:T(8,128)(2,1)} %copy.140), calls=%async_computation.6 | async-start | bytes 1048576 | tf_op jit(solution)/shard_map/all_to_all | solution.py:595
  326.3 71.6 %collective-permute-start.37 = (bf16[512,2736]{0,1:T(8,128)(2,1)}, bf16[512,2736]{0,1:T(8,128)(2,1)}, u32[]{:S(2)}, u32[]{:S(2)}) collective-permute-start(bf16[512,2736]{0,1:T(8,128)(2,1)} %convolution_convert_fusion.2), channel_id=1, source_target_pairs={{0,8},{8,0},{16,24},{24,16},{1,9},{9,1},{17,25},{25,17},{2,10},{10... | collective-permute-start | bytes 8405000 | tf_op jit(solution)/shard_map/ppermute | solution.py:539
  326.3 86.8 %collective-permute-start.32 = (bf16[512,2736]{0,1:T(8,128)(2,1)}, bf16[512,2736]{0,1:T(8,128)(2,1)}, u32[]{:S(2)}, u32[]{:S(2)}) collective-permute-start(bf16[512,2736]{0,1:T(8,128)(2,1)} %convolution_convert_fusion), channel_id=1, source_target_pairs={{0,8},{8,0},{16,24},{24,16},{1,9},{9,1},{17,25},{25,17},{2,10},{10... | collective-permute-start | bytes 8405000 | tf_op jit(solution)/shard_map/ppermute | solution.py:539
  330.2 98.7 %collective-permute-start.27 = (bf16[512,2736]{0,1:T(8,128)(2,1)}, bf16[512,2736]{0,1:T(8,128)(2,1)}, u32[]{:S(2)}, u32[]{:S(2)}) collective-permute-start(bf16[512,2736]{0,1:T(8,128)(2,1)} %convolution_convert_fusion.1), channel_id=1, source_target_pairs={{0,8},{8,0},{16,24},{24,16},{1,9},{9,1},{17,25},{25,17},{2,10},{10... | collective-permute-start | bytes 8405000 | tf_op jit(solution)/shard_map/ppermute | solution.py:539
  333.0 13.4 %collective-permute-start.22 = (bf16[128,1024]{1,0:T(8,128)(2,1)}, bf16[128,1024]{1,0:T(8,128)(2,1)}, u32[]{:S(2)}, u32[]{:S(2)}) collective-permute-start(bf16[128,1024]{1,0:T(8,128)(2,1)} %get-tuple-element.246), channel_id=1, source_target_pairs={{0,1},{1,0},{2,3},{3,2},{4,5},{5,4},{6,7},{7,6},{8,9},{9,8},{10,11... | collective-permute-start | bytes 786440 | tf_op jit(solution)/shard_map/ppermute | solution.py:539
  337.7 12.6 %collective-permute-start.17 = (bf16[128,1024]{1,0:T(8,128)(2,1)}, bf16[128,1024]{1,0:T(8,128)(2,1)}, u32[]{:S(2)}, u32[]{:S(2)}) collective-permute-start(bf16[128,1024]{1,0:T(8,128)(2,1)} %get-tuple-element.248), channel_id=1, source_target_pairs={{0,2},{1,3},{2,0},{3,1},{4,6},{5,7},{6,4},{7,5},{8,10},{9,11},{10,... | collective-permute-start | bytes 786440 | tf_op jit(solution)/shard_map/ppermute | solution.py:539
  340.9 18.3 %all-to-all-start.7 = ((bf16[8,256,128]{1,2,0:T(8,128)(2,1)}), bf16[8,256,128]{1,2,0:T(8,128)(2,1)S(1)}, u32[]{:S(2)}, u32[]{:S(2)}) async-start(bf16[8,256,128]{1,2,0:T(8,128)(2,1)} %copy.143), calls=%async_computation.7 | async-start | bytes 1048576 | tf_op jit(solution)/shard_map/all_to_all | solution.py:595
  348.3 33.7 %collective-permute-start.23 = (bf16[64,1024]{1,0:T(8,128)(2,1)}, bf16[64,1024]{1,0:T(8,128)(2,1)}, u32[]{:S(2)}, u32[]{:S(2)}) collective-permute-start(bf16[64,1024]{1,0:T(8,128)(2,1)} %get-tuple-element.268), channel_id=1, source_target_pairs={{0,2},{1,3},{2,0},{3,1},{4,6},{5,7},{6,4},{7,5},{8,10},{9,11},{10,... | collective-permute-start | bytes 393224 | tf_op jit(solution)/shard_map/ppermute | solution.py:539
  352.1 31.0 %collective-permute-start.18 = (bf16[64,1024]{1,0:T(8,128)(2,1)}, bf16[64,1024]{1,0:T(8,128)(2,1)}, u32[]{:S(2)}, u32[]{:S(2)}) collective-permute-start(bf16[64,1024]{1,0:T(8,128)(2,1)} %get-tuple-element.270), channel_id=1, source_target_pairs={{0,16},{8,24},{16,0},{24,8},{1,17},{9,25},{17,1},{25,9},{2,18},{10... | collective-permute-start | bytes 393224 | tf_op jit(solution)/shard_map/ppermute | solution.py:539
  366.3 15.0 %all-to-all-start.10 = ((f32[32,1,96]{2,1,0:T(1,128)}), f32[32,1,96]{2,1,0:T(1,128)S(1)}, u32[]{:S(2)}, u32[]{:S(2)}) async-start(f32[32,1,96]{2,1,0:T(1,128)} %bitcast.42), calls=%async_computation.10 | async-start | bytes 32768 | tf_op jit(solution)/shard_map/all_to_all | solution.py:672
  382.0 64.0 %collective-permute-start.10 = (bf16[512,1040]{0,1:T(8,128)(2,1)}, bf16[512,1040]{0,1:T(8,128)(2,1)}, u32[]{:S(2)}, u32[]{:S(2)}) collective-permute-start(bf16[512,1040]{0,1:T(8,128)(2,1)} %convolution_convert_fusion.6), channel_id=1, source_target_pairs={{0,8},{8,0},{16,24},{24,16},{1,9},{9,1},{17,25},{25,17},{2,10},{10... | collective-permute-start | bytes 3194888 | tf_op jit(solution)/shard_map/ppermute | solution.py:539
  396.3 41.2 %collective-permute-start.5 = (bf16[512,1024]{1,0:T(8,128)(2,1)}, bf16[512,1024]{1,0:T(8,128)(2,1)}, u32[]{:S(2)}, u32[]{:S(2)}) collective-permute-start(bf16[512,1024]{1,0:T(8,128)(2,1)} %convolution_convert_fusion.12), channel_id=1, source_target_pairs={{0,8},{8,0},{16,24},{24,16},{1,9},{9,1},{17,25},{25,17},{2,10},{10... | collective-permute-start | bytes 3145736 | tf_op jit(solution)/shard_map/ppermute | solution.py:539
  397.8 43.3 %collective-permute-start = (bf16[512,1024]{1,0:T(8,128)(2,1)}, bf16[512,1024]{1,0:T(8,128)(2,1)}, u32[]{:S(2)}, u32[]{:S(2)}) collective-permute-start(bf16[512,1024]{1,0:T(8,128)(2,1)} %convolution_convert_fusion.14), channel_id=1, source_target_pairs={{0,8},{8,0},{16,24},{24,16},{1,9},{9,1},{17,25},{25,17},{2,10},{10... | collective-permute-start | bytes 3145736 | tf_op jit(solution)/shard_map/ppermute | solution.py:539
  413.1 119.6 %collective-permute-start.38 = (bf16[256,2736]{0,1:T(8,128)(2,1)}, bf16[256,2736]{0,1:T(8,128)(2,1)}, u32[]{:S(2)}, u32[]{:S(2)}) collective-permute-start(bf16[256,2736]{0,1:T(8,128)(2,1)} %copy.168), channel_id=1, source_target_pairs={{0,16},{8,24},{16,0},{24,8},{1,17},{9,25},{17,1},{25,9},{2,18},{10... | collective-permute-start | bytes 4202504 | tf_op jit(solution)/shard_map/ppermute | solution.py:539
  429.0 118.0 %collective-permute-start.33 = (bf16[256,2736]{0,1:T(8,128)(2,1)}, bf16[256,2736]{0,1:T(8,128)(2,1)}, u32[]{:S(2)}, u32[]{:S(2)}) collective-permute-start(bf16[256,2736]{0,1:T(8,128)(2,1)} %copy.159), channel_id=1, source_target_pairs={{0,2},{1,3},{2,0},{3,1},{4,6},{5,7},{6,4},{7,5},{8,10},{9,11},{10,... | collective-permute-start | bytes 4202504 | tf_op jit(solution)/shard_map/ppermute | solution.py:539
  440.6 16.7 %collective-permute-start.6 = (bf16[256,1024]{1,0:T(8,128)(2,1)}, bf16[256,1024]{1,0:T(8,128)(2,1)}, u32[]{:S(2)}, u32[]{:S(2)}) collective-permute-start(bf16[256,1024]{1,0:T(8,128)(2,1)} %get-tuple-element.228), channel_id=1, source_target_pairs={{0,16},{8,24},{16,0},{24,8},{1,17},{9,25},{17,1},{25,9},{2,18},{10... | collective-permute-start | bytes 1572872 | tf_op jit(solution)/shard_map/ppermute | solution.py:539
  443.9 28.9 %collective-permute-start.1 = (bf16[256,1024]{1,0:T(8,128)(2,1)}, bf16[256,1024]{1,0:T(8,128)(2,1)}, u32[]{:S(2)}, u32[]{:S(2)}) collective-permute-start(bf16[256,1024]{1,0:T(8,128)(2,1)} %get-tuple-element.230), channel_id=1, source_target_pairs={{0,2},{1,3},{2,0},{3,1},{4,6},{5,7},{6,4},{7,5},{8,10},{9,11},{10,... | collective-permute-start | bytes 1572872 | tf_op jit(solution)/shard_map/ppermute | solution.py:539
  448.5 27.3 %collective-permute-start.11 = (bf16[256,1040]{0,1:T(8,128)(2,1)}, bf16[256,1040]{0,1:T(8,128)(2,1)}, u32[]{:S(2)}, u32[]{:S(2)}) collective-permute-start(bf16[256,1040]{0,1:T(8,128)(2,1)} %get-tuple-element.222), channel_id=1, source_target_pairs={{0,1},{1,0},{2,3},{3,2},{4,5},{5,4},{6,7},{7,6},{8,9},{9,8},{10,11... | collective-permute-start | bytes 1597448 | tf_op jit(solution)/shard_map/ppermute | solution.py:539
  457.3 103.3 %collective-permute-start.28 = (bf16[256,2736]{0,1:T(8,128)(2,1)}, bf16[256,2736]{0,1:T(8,128)(2,1)}, u32[]{:S(2)}, u32[]{:S(2)}) collective-permute-start(bf16[256,2736]{0,1:T(8,128)(2,1)} %copy.150), channel_id=1, source_target_pairs={{0,1},{1,0},{2,3},{3,2},{4,5},{5,4},{6,7},{7,6},{8,9},{9,8},{10,11... | collective-permute-start | bytes 4202504 | tf_op jit(solution)/shard_map/ppermute | solution.py:539
  472.8 24.4 %collective-permute-start.7 = (bf16[128,1024]{1,0:T(8,128)(2,1)S(1)}, bf16[128,1024]{1,0:T(8,128)(2,1)S(1)}, u32[]{:S(2)}, u32[]{:S(2)}) collective-permute-start(bf16[128,1024]{1,0:T(8,128)(2,1)S(1)} %get-tuple-element.250), channel_id=1, source_target_pairs={{0,1},{1,0},{2,3},{3,2},{4,5},{5,4},{6,7},{7,6},{8,9},{9,8},{10,11... | collective-permute-start | bytes 786440 | tf_op jit(solution)/shard_map/ppermute | solution.py:539
  475.7 22.0 %collective-permute-start.2 = (bf16[128,1024]{1,0:T(8,128)(2,1)S(1)}, bf16[128,1024]{1,0:T(8,128)(2,1)S(1)}, u32[]{:S(2)}, u32[]{:S(2)}) collective-permute-start(bf16[128,1024]{1,0:T(8,128)(2,1)S(1)} %get-tuple-element.252), channel_id=1, source_target_pairs={{0,16},{8,24},{16,0},{24,8},{1,17},{9,25},{17,1},{25,9},{2,18},{10... | collective-permute-start | bytes 786440 | tf_op jit(solution)/shard_map/ppermute | solution.py:539
  497.2 7.7 %collective-permute-start.12 = (bf16[128,1040]{0,1:T(8,128)(2,1)S(1)}, bf16[128,1040]{0,1:T(8,128)(2,1)S(1)}, u32[]{:S(2)}, u32[]{:S(2)}) collective-permute-start(bf16[128,1040]{0,1:T(8,128)(2,1)S(1)} %get-tuple-element.244), channel_id=1, source_target_pairs={{0,2},{1,3},{2,0},{3,1},{4,6},{5,7},{6,4},{7,5},{8,10},{9,11},{10,... | collective-permute-start | bytes 798728 | tf_op jit(solution)/shard_map/ppermute | solution.py:539
  497.7 8.9 %collective-permute-start.8 = (bf16[64,1024]{1,0:T(8,128)(2,1)S(1)}, bf16[64,1024]{1,0:T(8,128)(2,1)S(1)}, u32[]{:S(2)}, u32[]{:S(2)}) collective-permute-start(bf16[64,1024]{1,0:T(8,128)(2,1)S(1)} %get-tuple-element.272), channel_id=1, source_target_pairs={{0,2},{1,3},{2,0},{3,1},{4,6},{5,7},{6,4},{7,5},{8,10},{9,11},{10,... | collective-permute-start | bytes 393224 | tf_op jit(solution)/shard_map/ppermute | solution.py:539
  509.9 10.1 %collective-permute-start.9 = (bf16[32,1024]{1,0:T(8,128)(2,1)S(1)}, bf16[32,1024]{1,0:T(8,128)(2,1)S(1)}, u32[]{:S(2)}, u32[]{:S(2)}) collective-permute-start(bf16[32,1024]{1,0:T(8,128)(2,1)S(1)} %add_convert_fusion.60), channel_id=1, source_target_pairs={{0,4},{1,5},{2,6},{3,7},{4,0},{5,1},{6,2},{7,3},{8,12},{9,13},{10,... | collective-permute-start | bytes 196616 | tf_op jit(solution)/shard_map/ppermute | solution.py:539
  513.1 8.3 %collective-permute-start.4 = (bf16[32,1024]{1,0:T(8,128)(2,1)S(1)}, bf16[32,1024]{1,0:T(8,128)(2,1)S(1)}, u32[]{:S(2)}, u32[]{:S(2)}) collective-permute-start(bf16[32,1024]{1,0:T(8,128)(2,1)S(1)} %add_convert_fusion.62), channel_id=1, source_target_pairs={{0,4},{1,5},{2,6},{3,7},{4,0},{5,1},{6,2},{7,3},{8,12},{9,13},{10,... | collective-permute-start | bytes 196616 | tf_op jit(solution)/shard_map/ppermute | solution.py:539
  520.0 9.3 %collective-permute-start.14 = (bf16[32,1040]{0,1:T(8,128)(2,1)S(1)}, bf16[32,1040]{0,1:T(8,128)(2,1)S(1)}, u32[]{:S(2)}, u32[]{:S(2)}) collective-permute-start(bf16[32,1040]{0,1:T(8,128)(2,1)S(1)} %add_convert_fusion.28), channel_id=1, source_target_pairs={{0,4},{1,5},{2,6},{3,7},{4,0},{5,1},{6,2},{7,3},{8,12},{9,13},{10,... | collective-permute-start | bytes 199688 | tf_op jit(solution)/shard_map/ppermute | solution.py:539
  545.5 27.2 %collective-permute-start.39 = (bf16[128,2736]{0,1:T(8,128)(2,1)}, bf16[128,2736]{0,1:T(8,128)(2,1)}, u32[]{:S(2)}, u32[]{:S(2)}) collective-permute-start(bf16[128,2736]{0,1:T(8,128)(2,1)} %copy.171), channel_id=1, source_target_pairs={{0,1},{1,0},{2,3},{3,2},{4,5},{5,4},{6,7},{7,6},{8,9},{9,8},{10,11... | collective-permute-start | bytes 2101256 | tf_op jit(solution)/shard_map/ppermute | solution.py:539
  559.1 23.4 %collective-permute-start.34 = (bf16[128,2736]{0,1:T(8,128)(2,1)}, bf16[128,2736]{0,1:T(8,128)(2,1)}, u32[]{:S(2)}, u32[]{:S(2)}) collective-permute-start(bf16[128,2736]{0,1:T(8,128)(2,1)} %copy.162), channel_id=1, source_target_pairs={{0,16},{8,24},{16,0},{24,8},{1,17},{9,25},{17,1},{25,9},{2,18},{10... | collective-permute-start | bytes 2101256 | tf_op jit(solution)/shard_map/ppermute | solution.py:539
  572.7 18.0 %collective-permute-start.29 = (bf16[128,2736]{0,1:T(8,128)(2,1)}, bf16[128,2736]{0,1:T(8,128)(2,1)}, u32[]{:S(2)}, u32[]{:S(2)}) collective-permute-start(bf16[128,2736]{0,1:T(8,128)(2,1)} %copy.153), channel_id=1, source_target_pairs={{0,2},{1,3},{2,0},{3,1},{4,6},{5,7},{6,4},{7,5},{8,10},{9,11},{10,... | collective-permute-start | bytes 2101256 | tf_op jit(solution)/shard_map/ppermute | solution.py:539
  580.5 17.6 %collective-permute-start.40 = (bf16[64,2736]{1,0:T(8,128)(2,1)}, bf16[64,2736]{1,0:T(8,128)(2,1)}, u32[]{:S(2)}, u32[]{:S(2)}) collective-permute-start(bf16[64,2736]{1,0:T(8,128)(2,1)} %get-tuple-element.254), channel_id=1, source_target_pairs={{0,2},{1,3},{2,0},{3,1},{4,6},{5,7},{6,4},{7,5},{8,10},{9,11},{10,... | collective-permute-start | bytes 1050632 | tf_op jit(solution)/shard_map/ppermute | solution.py:539
  590.1 9.5 %collective-permute-start.35 = (bf16[64,2736]{1,0:T(8,128)(2,1)}, bf16[64,2736]{1,0:T(8,128)(2,1)}, u32[]{:S(2)}, u32[]{:S(2)}) collective-permute-start(bf16[64,2736]{1,0:T(8,128)(2,1)} %get-tuple-element.256), channel_id=1, source_target_pairs={{0,1},{1,0},{2,3},{3,2},{4,5},{5,4},{6,7},{7,6},{8,9},{9,8},{10,11... | collective-permute-start | bytes 1050632 | tf_op jit(solution)/shard_map/ppermute | solution.py:539
  597.5 7.5 %collective-permute-start.30 = (bf16[64,2736]{1,0:T(8,128)(2,1)S(1)}, bf16[64,2736]{1,0:T(8,128)(2,1)S(1)}, u32[]{:S(2)}, u32[]{:S(2)}) collective-permute-start(bf16[64,2736]{1,0:T(8,128)(2,1)S(1)} %get-tuple-element.258), channel_id=1, source_target_pairs={{0,16},{8,24},{16,0},{24,8},{1,17},{9,25},{17,1},{25,9},{2,18},{10... | collective-permute-start | bytes 1050632 | tf_op jit(solution)/shard_map/ppermute | solution.py:539
  599.1 13.8 %collective-permute-start.41 = (bf16[32,2736]{1,0:T(8,128)(2,1)S(1)}, bf16[32,2736]{1,0:T(8,128)(2,1)S(1)}, u32[]{:S(2)}, u32[]{:S(2)}) collective-permute-start(bf16[32,2736]{1,0:T(8,128)(2,1)S(1)} %add_convert_fusion.42), channel_id=1, source_target_pairs={{0,4},{1,5},{2,6},{3,7},{4,0},{5,1},{6,2},{7,3},{8,12},{9,13},{10,... | collective-permute-start | bytes 525320 | tf_op jit(solution)/shard_map/ppermute | solution.py:539
  600.6 14.9 %collective-permute-start.36 = (bf16[32,2736]{1,0:T(8,128)(2,1)S(1)}, bf16[32,2736]{1,0:T(8,128)(2,1)S(1)}, u32[]{:S(2)}, u32[]{:S(2)}) collective-permute-start(bf16[32,2736]{1,0:T(8,128)(2,1)S(1)} %add_convert_fusion.44), channel_id=1, source_target_pairs={{0,4},{1,5},{2,6},{3,7},{4,0},{5,1},{6,2},{7,3},{8,12},{9,13},{10,... | collective-permute-start | bytes 525320 | tf_op jit(solution)/shard_map/ppermute | solution.py:539
  605.0 12.3 %collective-permute-start.31 = (bf16[32,2736]{1,0:T(8,128)(2,1)S(1)}, bf16[32,2736]{1,0:T(8,128)(2,1)S(1)}, u32[]{:S(2)}, u32[]{:S(2)}) collective-permute-start(bf16[32,2736]{1,0:T(8,128)(2,1)S(1)} %add_convert_fusion.46), channel_id=1, source_target_pairs={{0,4},{1,5},{2,6},{3,7},{4,0},{5,1},{6,2},{7,3},{8,12},{9,13},{10,... | collective-permute-start | bytes 525320 | tf_op jit(solution)/shard_map/ppermute | solution.py:539
  (87 other events, 977.5 us)
